TPU v7x, 512 devices: a whole 4x8x8 slice. The times are simulated.
512 devices in a mesh: lat: 64 (over y, z), ma: 8 (over x, core).
Axes of the slice: x: 4, y: 8, z: 8, core: 2. Of those that a mesh axis runs over, the one named last changes fastest.
Arguments:
- pair_wave: int32 [360], replicated, may hold values from 0 to 359, each once
- legendre: bfloat16 [360, 640, 768], P('ma', 'lat'), may hold values from -0.0078125 to 0.0078125
- coefs: bfloat16 [360, 768, 168], P('ma', 'lat'), may hold values from -6 to 6
Outputs:
- noise: float32 [53760, 1440], P(('lat', 'ma'))
Inputs may be any that keep to these rules, and one draw needn't show every extreme that they name: Slot q holds wavenumbers pair_wave[q] and 719 - pair_wave[q]; every value appears once.
All inputs are finite; a program needn't handle non-finite values.
Results may differ from a plain program's by a relative error of at most 0.0003.
Values may be sent and summed in bfloat16 or wider, within the bound.
No kernel may reach another device: no remote copies, remote signals or barrier semaphores. Data moves between devices by JAX's collectives and lax.ppermute only.
A program may use at most 64 MiB of HBM per device.

v0:
```python
import math

import jax
import jax.numpy as jnp
from jax import lax
from jax.sharding import Mesh
from jax.sharding import PartitionSpec as P

DEG = 720
LON = 1440
CH = 84
LAT_DEV = 10
MA = ("ma_0", "ma_1")
LAT_MA = ("lat", "ma_0", "ma_1")


def split_up(shard, dim, count):
    before, after = (shard.shape[:dim], shard.shape[dim + 1 :])
    return jnp.moveaxis(shard.reshape(*before, count, -1, *after), dim, 0)


def in_order(pieces, dim):
    pieces = jnp.moveaxis(pieces, 0, dim)
    dims = pieces.shape
    return pieces.reshape(*dims[:dim], dims[dim] * dims[dim + 1], *dims[dim + 2 :])


def moved_by_axis(pieces, axes, turns):
    dims = [lax.axis_size(a) for a in axes]
    pieces = pieces.reshape(*dims, *pieces.shape[1:])
    for k in turns:
        pieces = lax.all_to_all(pieces, axes[k], split_axis=k, concat_axis=k, tiled=True)
    return pieces.reshape(-1, *pieces.shape[len(axes) :])


def exchange_by_axis(shard, axes, turns, split_dim, concat_dim):
    pieces = split_up(shard, split_dim, lax.axis_size(axes))
    return in_order(moved_by_axis(pieces, axes, turns), concat_dim)


def chain_table(table, wave_ids, degree_top):
    row_count = table.shape[2]
    row_ids = jnp.arange(row_count, dtype=jnp.int32)[None, :]
    split_row = (degree_top - wave_ids)[:, None]
    inside = row_ids < split_row
    outside = (row_ids >= split_row) & (row_ids <= degree_top)
    masks = jnp.stack([inside, outside], axis=1)
    return jnp.where(masks[:, :, None, :], table[:, None, :, :], jnp.zeros((), table.dtype))


def fourier_basis(pair_wave, degree_top, lon_count):
    orders = jnp.stack([pair_wave, degree_top - 1 - pair_wave], axis=1)
    positions = jnp.arange(lon_count, dtype=jnp.int32)
    phase_int = orders[:, :, None] * positions[None, None, :] % lon_count
    radians = 2.0 * math.pi / lon_count * phase_int.astype(jnp.float32)
    weight = jnp.where(orders == 0, 1.0, 2.0).astype(jnp.float32)[:, :, None]
    real_row = weight * jnp.cos(radians)
    imag_row = -weight * jnp.sin(radians)
    return jnp.stack([real_row, imag_row], axis=2).reshape(-1, lon_count)


def body(pair_wave, legendre, coefs):
    lat_count = lax.axis_size("lat")
    lat_place = lax.axis_index("lat")
    ma_place = lax.axis_index(MA)
    slot_count = coefs.shape[0]
    wave_ids = lax.dynamic_slice_in_dim(pair_wave, ma_place * slot_count, slot_count)
    per_device = (slot_count + lat_count - 1) // lat_count
    extra = per_device * lat_count - slot_count
    table_pad = jnp.concatenate(
        [legendre, jnp.zeros((extra,) + legendre.shape[1:], legendre.dtype)], axis=0
    )
    coefs_pad = jnp.concatenate([coefs, jnp.zeros((extra,) + coefs.shape[1:], coefs.dtype)], axis=0)
    waves_pad = jnp.concatenate([wave_ids, jnp.zeros((extra,), jnp.int32)], axis=0)
    tables_in, coefs_in = (
        lax.all_to_all(table_pad, "lat", split_axis=0, concat_axis=1, tiled=True),
        lax.all_to_all(coefs_pad, "lat", split_axis=0, concat_axis=1, tiled=True),
    )
    my_waves = lax.dynamic_slice_in_dim(waves_pad, lat_place * per_device, per_device)
    masked = chain_table(tables_in, my_waves, DEG)
    sums = jnp.einsum("qeir,qrc->qeic", masked, coefs_in, preferred_element_type=jnp.float32)
    returned = lax.all_to_all(sums, "lat", split_axis=2, concat_axis=0, tiled=True)
    spectra = returned[:slot_count]
    arranged = jnp.transpose(
        spectra.reshape(slot_count, 2, LAT_DEV, 2, CH), (0, 1, 3, 2, 4)
    ).reshape(slot_count, 2, 2, LAT_DEV * CH)
    exchanged = exchange_by_axis(arranged, MA, (1, 0), 3, 0)
    fourier_rows = exchanged.reshape(-1, exchanged.shape[3])
    synth_basis = fourier_basis(pair_wave, DEG, LON)
    return lax.dot_general(
        fourier_rows, synth_basis, (((0,), (0,)), ((), ())), precision=lax.Precision.HIGHEST
    )


def solution(mesh):
    split = Mesh(mesh.devices.reshape(mesh.shape["lat"], 4, 2), ("lat", "ma_0", "ma_1"))
    placed = (P(), P(MA, "lat", None), P(MA, "lat", None))
    return jax.shard_map(
        body, mesh=split, in_specs=placed, out_specs=P(LAT_MA, None), check_vma=False
    )
```

profile of v0, /device:TPU:1, one launch (start us, length us, event | category | flops | bytes accessed | tf_op | source)
XLA Modules:
  0.0 170.7 jit_solution(15079287082618436240)
XLA Ops:
  0.0 1.1 copy.42
  1.1 0.1 concatenate.18
  1.1 0.0 copy-start
  1.1 1.3 reshape.144
  2.4 17.1 %all-to-all-start.1 = ((bf16[64,2,1008]{2,1,0:T(2,128)(2,1)}), bf16[64,2,1008]{2,1,0:T(2,128)(2,1)S(1)}, u32[]{:S(2)}, u32[]{:S(2)}) async-start(bf16[64,2,1008]{2,1,0:T(2,128)(2,1)} %reshape.144), calls=%async_computation.1 | async-start | bytes 524288 | tf_op jit(solution)/shard_map/all_to_all | solution.py:77
  19.6 1.4 copy.41
  20.9 1.3 concatenate.17
  22.2 10.2 %all-to-all-done.1 = bf16[64,2,1008]{2,1,0:T(2,128)(2,1)S(1)} async-done(((bf16[64,2,1008]{2,1,0:T(2,128)(2,1)}), bf16[64,2,1008]{2,1,0:T(2,128)(2,1)S(1)}, u32[]{:S(2)}, u32[]{:S(2)}) %all-to-all-start.1) | async-done | bytes 258080 | tf_op jit(solution)/shard_map/all_to_all | solution.py:77
  32.4 5.6 %all-to-all-start = ((bf16[64,10,768]{2,1,0:T(8,128)(2,1)}), bf16[64,10,768]{2,1,0:T(8,128)(2,1)S(1)}, u32[]{:S(2)}, u32[]{:S(2)}) async-start(bf16[64,10,768]{2,1,0:T(8,128)(2,1)} %concatenate.17), calls=%async_computation | async-start | bytes 3145728 | tf_op jit(solution)/shard_map/all_to_all | solution.py:76
  38.1 0.0 copy-done
  38.1 0.1 dynamic_slice.6
  38.2 0.6 fusion.16
  38.7 0.7 compare_and_fusion
  39.4 0.7 reshape.145
  40.1 0.2 reshape.139
  40.3 34.3 %all-to-all-done = bf16[64,10,768]{2,1,0:T(8,128)(2,1)S(1)} async-done(((bf16[64,10,768]{2,1,0:T(8,128)(2,1)}), bf16[64,10,768]{2,1,0:T(8,128)(2,1)S(1)}, u32[]{:S(2)}, u32[]{:S(2)}) %all-to-all-start) | async-done | bytes 983072 | tf_op jit(solution)/shard_map/all_to_all | solution.py:76
  74.6 0.4 broadcast_in_dim.43
  75.0 0.8 fusion.8
  75.8 2.0 %copy.44 = f32[1,2,640,168]{3,1,0,2:T(2,128)} copy(f32[1,2,640,168]{2,3,1,0:T(8,128)S(1)} %fusion.8) | data formatting | bytes 1720320 | tf_op jit(solution)/shard_map/qeir,qrc->qeic/dot_general | solution.py:81
  77.9 10.3 %all-to-all-start.2 = ((f32[1,2,640,168]{3,1,0,2:T(2,128)}), f32[1,2,640,168]{3,1,0,2:T(2,128)S(1)}, u32[]{:S(2)}, u32[]{:S(2)}) async-start(f32[1,2,640,168]{3,1,0,2:T(2,128)} %copy.44), calls=%async_computation.2 | async-start | bytes 2621440 | tf_op jit(solution)/shard_map/all_to_all | solution.py:82
  88.3 21.3 %cosine_multiply_fusion = (f32[360,2,1,1440]{3,0,2,1:T(8,128)}, f32[360,2,1,1440]{3,0,2,1:T(8,128)}) fusion(s32[360,2]{0,1:T(2,128)S(1)} %pad_add_fusion, f32[360,2]{0,1:T(2,128)S(1)} %get-tuple-element.7, f32[360,2]{0,1:T(2,128)S(1)} %get-tuple-element.8), kind=kLoop, calls=%fused_computation.5 | loop fusion | flops 11404800 | bytes 8303040 | tf_op jit(solution)/shard_map/mul | solution.py:57
  109.6 9.3 %all-to-all-done.2 = f32[1,2,640,168]{3,1,0,2:T(2,128)S(1)} async-done(((f32[1,2,640,168]{3,1,0,2:T(2,128)}), f32[1,2,640,168]{3,1,0,2:T(2,128)S(1)}, u32[]{:S(2)}, u32[]{:S(2)}) %all-to-all-start.2) | async-done | bytes 860192 | tf_op jit(solution)/shard_map/all_to_all | solution.py:82
  118.9 0.3 slice.5
  119.2 1.2 reshape.140
  120.4 0.2 copy.52
  120.6 0.6 reshape_reshape.3
  121.2 0.4 copy.46
  121.6 9.1 %all_to_all.43 = f32[4,2,45,2,2,105]{5,4,3,2,0,1:T(2,128)S(1)} all-to-all(f32[4,2,45,2,2,105]{5,4,3,2,0,1:T(2,128)S(1)} %copy.46), channel_id=1, replica_groups=mesh['lat'=64,'ma_0'=4,'ma_1'=2] {'ma_1'}, dimensions={1} | all-to-all | bytes 1209600 | tf_op jit(solution)/shard_map/all_to_all | solution.py:32
  130.7 1.2 copy.47
  131.9 4.0 %all-to-all-start.4 = ((f32[4,2,45,2,2,105]{5,4,3,2,1,0:T(2,128)}), f32[4,2,45,2,2,105]{5,4,3,2,1,0:T(2,128)S(1)}, u32[]{:S(2)}, u32[]{:S(2)}) async-start(f32[4,2,45,2,2,105]{5,4,3,2,1,0:T(2,128)} %copy.47), calls=%async_computation.4 | async-start | bytes 1474560 | tf_op jit(solution)/shard_map/all_to_all | solution.py:32
  135.9 4.4 %pad_maximum_fusion = f32[360,2,2,1440]{3,0,2,1:T(8,128)S(1)} fusion(f32[360,2,1,1440]{3,0,2,1:T(8,128)} %get-tuple-element.6, f32[360,2,1,1440]{3,0,2,1:T(8,128)} %get-tuple-element.5), kind=kLoop, calls=%fused_computation | loop fusion | flops 2073600 | bytes 16588800 | tf_op jit(solution)/shard_map/stack | solution.py:59
  140.3 10.9 %copy.48 = f32[360,2,2,1440]{3,2,1,0:T(2,128)} copy(f32[360,2,2,1440]{3,0,2,1:T(8,128)S(1)} %pad_maximum_fusion) | data formatting | bytes 16588800 | tf_op jit(solution)/shard_map/stack | solution.py:59
  151.2 11.4 %reshape.142 = f32[1440,1440]{1,0:T(8,128)} reshape(f32[360,2,2,1440]{3,2,1,0:T(2,128)} %copy.48) | data formatting | bytes 16588800 | tf_op jit(solution)/shard_map/reshape | solution.py:59
  162.6 0.0 all-to-all-done.4
  162.6 8.1 %fusion.17 = f32[105,1440]{1,0:T(8,128)} fusion(f32[1440,105]{1,0:T(8,128)S(1)} %bitcast.24, f32[1440,1440]{1,0:T(8,128)} %reshape.142), kind=kOutput, calls=%fused_computation.28 | convolution fusion | flops 2612736000 | bytes 9504000 | tf_op jit(solution)/shard_map/dot_general | solution.py:90
  (6 shorter events, 0.0 us)
Async XLA Ops:
  1.1 36.9 %copy-start = (s32[360]{0:T(512)S(1)}, s32[360]{0:T(512)}, u32[]{:S(2)}) copy-start(s32[360]{0:T(512)} %param.3) | copy-start | bytes 4324
  2.4 30.0 %all-to-all-start.1 = ((bf16[64,2,1008]{2,1,0:T(2,128)(2,1)}), bf16[64,2,1008]{2,1,0:T(2,128)(2,1)S(1)}, u32[]{:S(2)}, u32[]{:S(2)}) async-start(bf16[64,2,1008]{2,1,0:T(2,128)(2,1)} %reshape.144), calls=%async_computation.1 | async-start | bytes 524288 | tf_op jit(solution)/shard_map/all_to_all | solution.py:77
  32.4 42.2 %all-to-all-start = ((bf16[64,10,768]{2,1,0:T(8,128)(2,1)}), bf16[64,10,768]{2,1,0:T(8,128)(2,1)S(1)}, u32[]{:S(2)}, u32[]{:S(2)}) async-start(bf16[64,10,768]{2,1,0:T(8,128)(2,1)} %concatenate.17), calls=%async_computation | async-start | bytes 3145728 | tf_op jit(solution)/shard_map/all_to_all | solution.py:76
  77.9 41.0 %all-to-all-start.2 = ((f32[1,2,640,168]{3,1,0,2:T(2,128)}), f32[1,2,640,168]{3,1,0,2:T(2,128)S(1)}, u32[]{:S(2)}, u32[]{:S(2)}) async-start(f32[1,2,640,168]{3,1,0,2:T(2,128)} %copy.44), calls=%async_computation.2 | async-start | bytes 2621440 | tf_op jit(solution)/shard_map/all_to_all | solution.py:82
  131.9 30.7 %all-to-all-start.4 = ((f32[4,2,45,2,2,105]{5,4,3,2,1,0:T(2,128)}), f32[4,2,45,2,2,105]{5,4,3,2,1,0:T(2,128)S(1)}, u32[]{:S(2)}, u32[]{:S(2)}) async-start(f32[4,2,45,2,2,105]{5,4,3,2,1,0:T(2,128)} %copy.47), calls=%async_computation.4 | async-start | bytes 1474560 | tf_op jit(solution)/shard_map/all_to_all | solution.py:32
where the time goes:
time: 172 us; the launch traced here: 171 us
  waiting for transfers between devices  53.9 us (31%)
  starting transfers between devices  37.1 us (22%)
  local copies, waits for them, and re-layouts  34.5 us (20%)
  other arithmetic  27 us (16%)
  blocking collectives  9.12 us (5%)
  matrix products  8.94 us (5%)
    all_to_all x1, waiting for transfers between devices, body(): lax.all_to_all(table_pad, 'lat', split_axis=0, concat_axis=1, tiled=True)  34.3 us
    mul x1, other arithmetic, fourier_basis(): real_row = weight * jnp.cos(radians)  21.3 us
    all_to_all x1, starting transfers between devices, body(): lax.all_to_all(coefs_pad, 'lat', split_axis=0, concat_axis=1, tiled=True)  17.1 us
    reshape x1, local copies, waits for them, and re-layouts, fourier_basis(): return jnp.stack([real_row, imag_row], axis=2).reshape(-1, lon_count)  11.4 us
    another operation x1, local copies, waits for them, and re-layouts, fourier_basis(): return jnp.stack([real_row, imag_row], axis=2).reshape(-1, lon_count)  10.9 us
    all_to_all x1, starting transfers between devices, body(): lax.all_to_all(sums, 'lat', split_axis=2, concat_axis=0, tiled=True)  10.3 us
    all_to_all x1, waiting for transfers between devices, body(): lax.all_to_all(coefs_pad, 'lat', split_axis=0, concat_axis=1, tiled=True)  10.2 us
    all_to_all x1, waiting for transfers between devices, body(): lax.all_to_all(sums, 'lat', split_axis=2, concat_axis=0, tiled=True)  9.33 us
  transfers between devices with their start and end apart: 4, of which 3 were waited for; matrix products, arithmetic and copies ran while one was open for 31% of the time, Pallas kernels for 0%

commit v1 on v0

v1 whole, which is shorter than its diff:
```python
import math

import jax
import jax.numpy as jnp
from jax import lax
from jax.sharding import Mesh
from jax.sharding import PartitionSpec as P

DEG = 720
LON = 1440
HALF = LON // 2
CH = 84
LAT_DEV = 10
N_MA = 8
PART = LAT_DEV * CH // N_MA
LANES = 128
LAT = ("y", "z")
MA = ("x", "core")
ALL = ("y", "z", "x", "core")
TOP = 14


def packed(legendre, coefs):
    slots = legendre.shape[0]
    weights = legendre.reshape(slots, -1, LANES)
    main = coefs[:, :, :LANES]
    rest = coefs[:, :, LANES:]
    rest = jnp.transpose(rest.reshape(slots, 3, 4, -1), (0, 2, 1, 3)).reshape(slots, 4, -1)
    rest = jnp.pad(rest, ((0, 0), (0, 0), (0, LANES - rest.shape[2])))
    return jnp.concatenate([weights, main, rest], axis=1)


def unpacked(rows, lat_rows, coef_rows, columns):
    devices = rows.shape[0]
    at = lat_rows * 6
    weights = rows[:, :at].reshape(devices * lat_rows, 6 * LANES)
    main = rows[:, at : at + coef_rows]
    width = columns - LANES
    rest = rows[:, at + coef_rows :, : 3 * width].reshape(devices, 4, 3, width)
    rest = jnp.transpose(rest, (0, 2, 1, 3)).reshape(devices, coef_rows, width)
    coefs = jnp.concatenate([main, rest], axis=2).reshape(devices * coef_rows, columns)
    return weights, coefs


def in_two(full):
    high = lax.reduce_precision(full, 8, 7)
    return high.astype(jnp.bfloat16), (full - high).astype(jnp.bfloat16)


def basis(pair_wave, slots):
    first = pair_wave.reshape(N_MA, slots).T.reshape(-1)
    other = DEG - 1 - first
    is_even = first % 2 == 0
    waves = jnp.stack([jnp.where(is_even, first, other), jnp.where(is_even, other, first)])
    positions = jnp.arange(HALF, dtype=jnp.int32)
    phase = waves[:, :, None] * positions[None, None, :] % LON
    radians = 2.0 * math.pi / LON * phase.astype(jnp.float32)
    weight = jnp.where(waves == 0, 1.0, 2.0).astype(jnp.float32)[:, :, None]
    full = jnp.stack([weight * jnp.cos(radians), -weight * jnp.sin(radians)], axis=1)
    return in_two(full)


def body(pair_wave, legendre, coefs):
    lat_count = lax.axis_size(LAT)
    lat_place = lax.axis_index(LAT)
    ma_place = lax.axis_index(MA)
    slots, lat_rows, degree_rows = legendre.shape
    coef_rows, columns = coefs.shape[1:]
    sent = packed(legendre, coefs)
    sent = jnp.pad(sent, ((0, lat_count - slots), (0, 0), (0, 0)))
    sent = sent.reshape(lat_count, -1, 4, LANES)
    got = lax.all_to_all(sent, LAT, split_axis=0, concat_axis=0, tiled=True)
    weights, packed_coefs = unpacked(
        got.reshape(lat_count, -1, LANES), lat_rows, coef_rows, columns
    )
    slot = ma_place * slots + jnp.minimum(lat_place, slots - 1)
    wave = lax.dynamic_index_in_dim(pair_wave, slot, keepdims=False)
    row_ids = jnp.arange(degree_rows, dtype=jnp.int32)[:, None]
    inside = row_ids < DEG - wave
    outside = (row_ids >= DEG - wave) & (row_ids <= DEG)
    is_even = wave % 2 == 0
    zero = jnp.zeros((), coefs.dtype)
    even = jnp.where(jnp.where(is_even, inside, outside), packed_coefs, zero)
    odd = jnp.where(jnp.where(is_even, outside, inside), packed_coefs, zero)
    sums = jnp.dot(
        weights, jnp.concatenate([even, odd], axis=1), preferred_element_type=jnp.float32
    )
    largest = jnp.max(jnp.abs(sums))
    power = jnp.clip(jnp.floor(jnp.log2(jnp.maximum(largest, 1e-30))), -100.0, 100.0)
    parts = jnp.transpose(sums.reshape(lat_count, lat_rows, 4, CH), (0, 2, 1, 3))
    parts = parts.reshape(lat_count, 4, N_MA, PART) * jnp.exp2(TOP - power)
    parts = jnp.transpose(parts, (0, 2, 1, 3)).reshape(lat_count * N_MA, 4, PART)
    note = jnp.broadcast_to(power, (lat_count * N_MA, 4, LANES - PART))
    parts = jnp.concatenate([parts, note], axis=2).astype(jnp.float16)
    spectra = lax.all_to_all(parts, ALL, split_axis=0, concat_axis=0, tiled=True)
    spectra = spectra[: slots * N_MA].astype(jnp.float32)
    spectra = spectra * jnp.exp2(spectra[:, :, PART:][:, :, :1] - TOP)
    spectra = spectra[:, :, :PART]
    high, low = in_two(spectra)
    base_high, base_low = basis(pair_wave, slots)

    def times(h, b, parity):
        return lax.dot_general(
            h[:, 2 * parity : 2 * parity + 2],
            b[parity],
            (((1, 0), (0, 1)), ((), ())),
            preferred_element_type=jnp.float32,
        )

    halves = [
        times(high, base_high, k) + times(low, base_high, k) + times(high, base_low, k)
        for k in range(2)
    ]
    return jnp.concatenate([halves[0] + halves[1], halves[0] - halves[1]], axis=1)


def solution(mesh):
    split = Mesh(mesh.devices.reshape(8, mesh.shape["lat"] // 8, 4, 2), ALL)
    placed = (P(), P(MA, LAT, None), P(MA, LAT, None))
    return jax.shard_map(
        body, mesh=split, in_specs=placed, out_specs=P(ALL, None), check_vma=False
    )
```

time: 172 us -> 105 us (0.61)
  local copies, waits for them, and re-layouts: 34.5 us -> 13.5 us
  waiting for transfers between devices: 53.9 us -> 38.1 us
  other arithmetic: 27 us -> 13.2 us
  blocking collectives: 9.12 us -> 0 us
  matrix products: 8.94 us -> 3.44 us
  starting transfers between devices: 37.1 us -> 32.2 us
  between operations: 0.18 us -> 3.71 us
    all_to_all x4 -> x2, waiting for transfers between devices: 53.9 us -> 38.1 us  [the longest x1 27.3 us: body(): got = lax.all_to_all(sent, LAT, split_axis=0, concat_axis=0, tiled=True)]
    mul x1, other arithmetic: 21.3 us -> 9.39 us  [basis(): weight * jnp.cos(radians)]
    another operation x5 -> x1, local copies, waits for them, and re-layouts: 11.7 us -> 0.47 us  [the longest x1 10.9 us: fourier_basis(): return jnp.stack([real_row, imag_row], axis=2).reshape(-1, lon_count)]
    all_to_all x1 -> x0, blocking collectives: 9.12 us -> none  [moved_by_axis(): lax.all_to_all(pieces, axes[k], split_axis=k, concat_axis=k, tiled=True)]
    reshape x4 -> x8, local copies, waits for them, and re-layouts: 13.1 us -> 4.14 us  [the longest x1 2.03 us: body(): sent = sent.reshape(lat_count, -1, 4, LANES)]
    dot_general x2 -> x7, matrix products: 8.94 us -> 3.44 us  [the longest x6 2.07 us: times(): lax.dot_general(h[:, 2 * parity:2 * parity + 2], b[parity], (((1, 0), (0,...]
    all_to_all x4 -> x2, starting transfers between devices: 37.1 us -> 32.2 us  [the longest x1 17.1 us: body(): got = lax.all_to_all(sent, LAT, split_axis=0, concat_axis=0, tiled=True)]
    another operation x2, other arithmetic: 4.39 us -> 0.09 us  [the longest x1 4.38 us: fourier_basis(): return jnp.stack([real_row, imag_row], axis=2).reshape(-1, lon_count)]
  transfers between devices with their start and end apart: 4 -> 2, of which waited for: 3 -> 2; matrix products, arithmetic and copies ran while one was open for 31% -> 12% of each run, Pallas kernels for 0% -> 0%
where the time goes in v1:
time: 105 us; the launch traced here: 104 us
  waiting for transfers between devices  38.1 us (36%)
  starting transfers between devices  32.2 us (31%)
  local copies, waits for them, and re-layouts  13.5 us (13%)
  other arithmetic  13.2 us (13%)
  between operations  3.71 us (4%)
  matrix products  3.44 us (3%)
    all_to_all x1, waiting for transfers between devices, body(): got = lax.all_to_all(sent, LAT, split_axis=0, concat_axis=0, tiled=True)  27.3 us
    all_to_all x1, starting transfers between devices, body(): got = lax.all_to_all(sent, LAT, split_axis=0, concat_axis=0, tiled=True)  17.1 us
    all_to_all x1, starting transfers between devices, body(): lax.all_to_all(parts, ALL, split_axis=0, concat_axis=0, tiled=True)  15.1 us
    all_to_all x1, waiting for transfers between devices, body(): lax.all_to_all(parts, ALL, split_axis=0, concat_axis=0, tiled=True)  10.8 us
    mul x1, other arithmetic, basis(): weight * jnp.cos(radians)  9.39 us
    unnamed x10, local copies, waits for them, and re-layouts  3.42 us
    convert_element_type x2, other arithmetic, in_two(): return (high.astype(jnp.bfloat16), (full - high).astype(jnp.bfloat16))  2.13 us
  transfers between devices with their start and end apart: 2, of which 2 were waited for; matrix products, arithmetic and copies ran while one was open for 12% of the time, Pallas kernels for 0%

profile of v1, /device:TPU:1, one launch (start us, length us, event | category | flops | bytes accessed | tf_op | source)
XLA Modules:
  0.0 104.2 jit_solution(12783467355637196647)
XLA Ops:
  0.0 0.0 slice-start
  0.0 0.0 slice-start.1
  0.0 1.4 %copy.19 = bf16[45,10,768]{2,1,0:T(8,128)(2,1)S(1)} copy(bf16[45,10,768]{2,0,1:T(8,128)(2,1)} %param.4) | data formatting | bytes 1382400 | tf_op args[1]
  1.4 0.6 reshape.244
  2.1 0.0 slice-done
  2.1 0.0 slice-done.1
  2.1 0.2 copy.21
  2.3 0.1 copy.22
  2.4 0.2 fusion.11
  2.6 0.2 copy.39
  2.9 0.2 pad.11.clone
  3.1 0.0 copy-start.1
  3.1 2.0 %copy.24 = bf16[64,19,4,128]{3,2,1,0:T(4,128)(2,1)} copy(bf16[64,19,4,128]{3,0,2,1:T(8,128)(2,1)S(1)} %bitcast.65) | data formatting | bytes 2490368 | tf_op jit(solution)/shard_map/reshape | solution.py:71
  5.2 17.1 %all-to-all-start = ((bf16[64,19,4,128]{3,2,1,0:T(4,128)(2,1)}), bf16[64,19,4,128]{3,2,1,0:T(4,128)(2,1)S(1)}, u32[]{:S(2)}, u32[]{:S(2)}) async-start(bf16[64,19,4,128]{3,2,1,0:T(4,128)(2,1)} %copy.24), calls=%async_computation | async-start | bytes 2490368 | tf_op jit(solution)/shard_map/all_to_all | solution.py:72
  22.3 0.0 copy-done.1
  22.3 0.6 dynamic_slice.4
  24.9 0.1 reshape.252
  25.6 0.1 copy.35
  25.7 0.1 reshape.253
  25.8 27.3 %all-to-all-done = bf16[64,19,4,128]{3,2,1,0:T(4,128)(2,1)S(1)} async-done(((bf16[64,19,4,128]{3,2,1,0:T(4,128)(2,1)}), bf16[64,19,4,128]{3,2,1,0:T(4,128)(2,1)S(1)}, u32[]{:S(2)}, u32[]{:S(2)}) %all-to-all-start) | async-done | bytes 1245216 | tf_op jit(solution)/shard_map/all_to_all | solution.py:72
  53.1 0.3 copy.25
  53.4 0.1 slice.70
  53.5 0.1 copy.27
  53.7 0.1 copy.28
  53.8 0.2 copy.29
  54.0 0.6 copy.26
  54.6 0.9 reshape.249
  55.5 0.3 broadcast_select_fusion.1
  55.8 1.4 %abs_reduce_fusion = (f32[]{:T(128)}, f32[640,336]{0,1:T(8,128)S(1)}) fusion(bf16[640,768]{1,0:T(8,128)(2,1)S(1)} %reshape.249, bf16[768,168]{1,0:T(8,128)(2,1)S(1)} %get-tuple-element.12, bf16[768,168]{1,0:T(8,128)(2,1)S(1)} %get-tuple-element.11), kind=kOutput, calls=%fused_computation.33 | convolution fusion | flops 331763712 | bytes 2359300 | tf_op jit(solution)/shard_map/dot_general | solution.py:85
  57.9 0.1 multiply_convert_fusion
  58.0 0.5 copy.30
  58.5 0.4 mul.110
  58.9 0.3 copy.31
  59.3 1.0 mul.112
  60.3 0.1 copy_bitcast_fusion
  60.4 0.4 copy.40
  60.8 1.1 %concatenate.32.clone = f16[512,4,128]{2,1,0:T(4,128)(2,1)} pad(f16[512,4,105]{2,1,0:T(4,128)(2,1)S(1)} %copy.40, f16[]{:T(256)S(6)} %convert.12), padding=0_0x0_0x0_23 | pad | bytes 954370 | tf_op jit(solution)/shard_map/concatenate | solution.py:94
  62.0 15.1 %all-to-all-start.1 = ((f16[512,4,128]{2,1,0:T(4,128)(2,1)}), f16[512,4,128]{2,1,0:T(4,128)(2,1)S(1)}, u32[]{:S(2)}, u32[]{:S(2)}) async-start(f16[512,4,128]{2,1,0:T(4,128)(2,1)} %concatenate.32.clone), calls=%async_computation.1 | async-start | bytes 1048576 | tf_op jit(solution)/shard_map/all_to_all | solution.py:95
  77.1 9.4 %cosine_multiply_fusion = (f32[2,1,360,720]{3,2,1,0:T(8,128)S(1)}, f32[2,1,360,720]{3,2,1,0:T(8,128)S(1)}) fusion(s32[2,360]{1,0:T(2,128)S(1)} %pad_add_fusion, f32[2,360]{1,0:T(2,128)S(1)} %get-tuple-element.15, f32[2,360]{1,0:T(2,128)S(1)} %get-tuple-element.16), kind=kLoop, calls=%fused_computation.8 | loop fusion | flops 5702400 | bytes 4155840 | tf_op jit(solution)/shard_map/mul | solution.py:59
  86.5 2.1 %reduce-precision_convert_fusion = (bf16[2,2,360,720]{3,2,1,0:T(8,128)(2,1)S(1)}, bf16[2,2,360,720]{3,2,1,0:T(8,128)(2,1)}) fusion(f32[2,1,360,720]{3,2,1,0:T(8,128)S(1)} %get-tuple-element.14, f32[2,1,360,720]{3,2,1,0:T(8,128)S(1)} %get-tuple-element.13), kind=kLoop, calls=%fused_computation.1 | loop fusion | flops 5184000 | bytes 8294400 | tf_op jit(solution)/shard_map/convert_element_type | solution.py:47
  88.6 10.8 %all-to-all-done.1 = f16[512,4,128]{2,1,0:T(4,128)(2,1)S(1)} async-done(((f16[512,4,128]{2,1,0:T(4,128)(2,1)}), f16[512,4,128]{2,1,0:T(4,128)(2,1)S(1)}, u32[]{:S(2)}, u32[]{:S(2)}) %all-to-all-start.1) | async-done | bytes 524320 | tf_op jit(solution)/shard_map/all_to_all | solution.py:95
  99.4 0.1 slice.73
  99.6 0.4 copy.38
  100.0 0.1 convert_element_type.34
  100.1 0.1 reduce-precision_convert_fusion.1
  100.1 0.0 copy-start
  100.1 0.4 convolution_bitcast_fusion.4
  100.5 0.3 convolution_bitcast_fusion.1
  100.9 0.9 copy-done
  101.8 0.3 convolution_bitcast_fusion.3
  102.1 0.3 convolution_bitcast_fusion
  102.4 0.3 fusion.10
  102.8 0.4 fusion.27
  103.2 1.0 pad_maximum_fusion.1
  (11 shorter events, 0.2 us)
Async XLA Ops:
  0.0 2.1 %slice-start = ((bf16[45,12,168]{2,0,1:T(8,128)(2,1)}), bf16[45,12,128]{2,0,1:T(8,128)(2,1)S(1)}, s32[]{:S(2)}) async-start(bf16[45,12,168]{2,0,1:T(8,128)(2,1)} %param.5), calls=%async_computation.2 | async-start | bytes 294912 | tf_op jit(solution)/shard_map/slice | solution.py:26
  0.0 2.1 %slice-start.1 = ((bf16[45,12,168]{2,0,1:T(8,128)(2,1)}), bf16[45,12,40]{2,0,1:T(8,128)(2,1)S(1)}, s32[]{:S(2)}) async-start(bf16[45,12,168]{2,0,1:T(8,128)(2,1)} %param.5), calls=%async_computation.3 | async-start | bytes 294912 | tf_op jit(solution)/shard_map/slice | solution.py:27
  3.1 19.2 %copy-start.1 = (s32[360]{0:T(512)S(1)}, s32[360]{0:T(512)}, u32[]{:S(2)}) copy-start(s32[360]{0:T(512)} %param.3) | copy-start | bytes 4324
  5.2 47.9 %all-to-all-start = ((bf16[64,19,4,128]{3,2,1,0:T(4,128)(2,1)}), bf16[64,19,4,128]{3,2,1,0:T(4,128)(2,1)S(1)}, u32[]{:S(2)}, u32[]{:S(2)}) async-start(bf16[64,19,4,128]{3,2,1,0:T(4,128)(2,1)} %copy.24), calls=%async_computation | async-start | bytes 2490368 | tf_op jit(solution)/shard_map/all_to_all | solution.py:72
  62.0 37.5 %all-to-all-start.1 = ((f16[512,4,128]{2,1,0:T(4,128)(2,1)}), f16[512,4,128]{2,1,0:T(4,128)(2,1)S(1)}, u32[]{:S(2)}, u32[]{:S(2)}) async-start(f16[512,4,128]{2,1,0:T(4,128)(2,1)} %concatenate.32.clone), calls=%async_computation.1 | async-start | bytes 1048576 | tf_op jit(solution)/shard_map/all_to_all | solution.py:95
  100.1 1.6 %copy-start = (bf16[2,2,360,720]{3,2,1,0:T(8,128)(2,1)S(1)}, bf16[2,2,360,720]{3,2,1,0:T(8,128)(2,1)}, u32[]{:S(2)}) copy-start(bf16[2,2,360,720]{3,2,1,0:T(8,128)(2,1)} %get-tuple-element.8) | copy-start | bytes 6220804

commit v2 on v1

v2 whole, which is shorter than its diff:
```python
import functools
import math

import jax
import jax.numpy as jnp
from jax import lax
from jax.experimental import pallas as pl
from jax.experimental.pallas import tpu as pltpu
from jax.sharding import Mesh
from jax.sharding import PartitionSpec as P

DEG = 720
LON = 1440
HALF = LON // 2
CH = 84
LAT_DEV = 10
N_MA = 8
PART = LAT_DEV * CH // N_MA
LANES = 128
LAT = ("y", "z")
MA = ("x", "core")
ALL = ("y", "z", "x", "core")
TOP = 14


def sums_kernel(wave_ref, got_ref, out_ref, wide_ref, weights_ref, real_ref, imag_ref, sums_ref, turned_ref, *, lat_count, lat_rows, coef_rows):
    chunk = got_ref.shape[0] // lat_count
    blocks = DEG // LANES + 1
    depth = lat_count * coef_rows
    wide_ref[...] = got_ref[...].astype(jnp.float32)
    for i in range(lat_rows):
        for b in range(blocks):
            piece = wide_ref[pl.ds(i * blocks + b, lat_count, stride=chunk), :]
            weights_ref[i * lat_count : (i + 1) * lat_count, b * LANES : (b + 1) * LANES] = piece.astype(jnp.bfloat16)
    at = lat_rows * blocks
    tail = 2 * CH - LANES
    lane = lax.broadcasted_iota(jnp.int32, (lat_count, LANES), 1)
    for k in range(coef_rows):
        main = wide_ref[pl.ds(at + k, lat_count, stride=chunk), :]
        rest = wide_ref[pl.ds(at + coef_rows + k % 4, lat_count, stride=chunk), :]
        split = LANES - CH
        moved = pltpu.roll(main, LANES - CH, 1)
        rest = pltpu.roll(rest, (split - tail * (k // 4)) % LANES, 1)
        imag = jnp.where(lane < split, moved, rest)
        real_ref[pl.ds(k, lat_count, stride=coef_rows), :] = jnp.where(lane < CH, main, 0.0)
        imag_ref[pl.ds(k, lat_count, stride=coef_rows), :] = jnp.where(lane < CH, imag, 0.0)
    wave = wave_ref[0]
    row = lax.broadcasted_iota(jnp.int32, (depth, 2 * LANES), 0)
    inside = row < DEG - wave
    outside = jnp.logical_and(row >= DEG - wave, row <= DEG)
    both = jnp.concatenate([real_ref[...], imag_ref[...]], axis=1)
    is_even = wave % 2 == 0
    first = jnp.where(inside, both, 0.0)
    second = jnp.where(outside, both, 0.0)
    even = jnp.where(is_even, first, second).astype(jnp.bfloat16)
    odd = jnp.where(is_even, second, first).astype(jnp.bfloat16)
    weights = weights_ref[...]
    even = jnp.dot(weights, even, preferred_element_type=jnp.float32)
    odd = jnp.dot(weights, odd, preferred_element_type=jnp.float32)
    sums_ref[:, : 2 * LANES] = even
    sums_ref[:, 2 * LANES :] = odd
    largest = jnp.maximum(jnp.max(jnp.abs(even)), jnp.max(jnp.abs(odd)))
    largest = jnp.maximum(jnp.full((lat_count, LANES), largest, jnp.float32), 1e-30)
    power = jnp.clip(jnp.floor(jnp.log2(largest)), -100.0, 100.0)
    scale = jnp.exp2(TOP - power)
    pitch = turned_ref.shape[0] // lat_count
    for a in range(N_MA):
        i, off = divmod(a * PART, CH)
        for he in range(4):
            cols = slice(he * LANES, (he + 1) * LANES)
            near = sums_ref[i * lat_count : (i + 1) * lat_count, cols]
            far = sums_ref[(i + 1) * lat_count : (i + 2) * lat_count, cols]
            if off:
                near = pltpu.roll(near, LANES - off, 1)
            far = pltpu.roll(far, CH - off, 1)
            value = jnp.where(lane < CH - off, near, far) * scale
            value = jnp.where(lane < PART, value, power)
            turned_ref[pl.ds(a * 4 + he, lat_count, stride=pitch), :] = value
    rows = 4 * N_MA
    for l in range(lat_count):
        out_ref[l * rows : (l + 1) * rows, :] = turned_ref[l * pitch : l * pitch + rows, :]


def sums_call(wave, got, lat_count, lat_rows, coef_rows):
    blocks = DEG // LANES + 1
    vm = pltpu.VMEM
    return pl.pallas_call(
        functools.partial(sums_kernel, lat_count=lat_count, lat_rows=lat_rows, coef_rows=coef_rows),
        out_shape=pltpu.VMEM((lat_count * N_MA * 4, LANES), jnp.float32),
        in_specs=[pl.BlockSpec(memory_space=pltpu.SMEM), pl.BlockSpec(memory_space=vm)],
        out_specs=pl.BlockSpec(memory_space=vm),
        scratch_shapes=[
            vm(got.shape, jnp.float32),
            vm((lat_count * lat_rows, blocks * LANES), jnp.bfloat16),
            vm((lat_count * coef_rows, LANES), jnp.float32),
            vm((lat_count * coef_rows, LANES), jnp.float32),
            vm((lat_count * lat_rows, 4 * LANES), jnp.float32),
            vm((lat_count * (4 * N_MA + 4), LANES), jnp.float32),
        ],
    )(wave, got)


def pack_kernel(legendre_ref, coefs_ref, out_ref, wide_ref):
    lat_rows, slots, degree_rows = legendre_ref.shape
    coef_rows = coefs_ref.shape[0]
    blocks = degree_rows // LANES
    chunk = lat_rows * blocks + coef_rows + 4
    for i in range(lat_rows):
        for b in range(blocks):
            piece = legendre_ref[i, :, b * LANES : (b + 1) * LANES].astype(jnp.float32)
            wide_ref[pl.ds(i * blocks + b, slots, stride=chunk), :] = piece
    at = lat_rows * blocks
    tail = 2 * CH - LANES
    for k in range(coef_rows):
        wide_ref[pl.ds(at + k, slots, stride=chunk), :] = coefs_ref[k, :, :LANES].astype(jnp.float32)
    for t in range(4):
        parts = [coefs_ref[t + 4 * j, :, LANES:].astype(jnp.float32) for j in range(3)]
        parts.append(jnp.zeros((slots, LANES - 3 * tail), jnp.float32))
        wide_ref[pl.ds(at + coef_rows + t, slots, stride=chunk), :] = jnp.concatenate(parts, axis=1)
    full = slots * chunk
    out_ref[:full, :] = wide_ref[...].astype(jnp.bfloat16)
    out_ref[full:, :] = jnp.zeros((out_ref.shape[0] - full, LANES), jnp.bfloat16)


def pack_call(legendre, coefs, lat_count):
    slots, lat_rows, degree_rows = legendre.shape
    coef_rows = coefs.shape[1]
    chunk = lat_rows * degree_rows // LANES + coef_rows + 4
    vm = pltpu.VMEM
    return pl.pallas_call(
        pack_kernel,
        out_shape=jax.ShapeDtypeStruct((lat_count * chunk, LANES), jnp.bfloat16),
        in_specs=[pl.BlockSpec(memory_space=vm)] * 2,
        out_specs=pl.BlockSpec(memory_space=vm),
        scratch_shapes=[vm((slots * chunk, LANES), jnp.float32)],
    )(jnp.transpose(legendre, (1, 0, 2)), jnp.transpose(coefs, (1, 0, 2)))


def in_two(full):
    high = lax.reduce_precision(full, 8, 7)
    return high.astype(jnp.bfloat16), (full - high).astype(jnp.bfloat16)


def basis(pair_wave, slots):
    first = pair_wave.reshape(N_MA, slots).T.reshape(-1)
    other = DEG - 1 - first
    is_even = first % 2 == 0
    waves = jnp.stack([jnp.where(is_even, first, other), jnp.where(is_even, other, first)])
    positions = jnp.arange(HALF, dtype=jnp.int32)
    phase = waves[:, :, None] * positions[None, None, :] % LON
    radians = 2.0 * math.pi / LON * phase.astype(jnp.float32)
    weight = jnp.where(waves == 0, 1.0, 2.0).astype(jnp.float32)[:, :, None]
    full = jnp.stack([weight * jnp.cos(radians), -weight * jnp.sin(radians)], axis=1)
    return in_two(full)


def body(pair_wave, legendre, coefs):
    lat_count = lax.axis_size(LAT)
    lat_place = lax.axis_index(LAT)
    ma_place = lax.axis_index(MA)
    slots, lat_rows = legendre.shape[:2]
    coef_rows = coefs.shape[1]
    sent = pack_call(legendre, coefs, lat_count).reshape(lat_count, -1, 4, LANES)
    got = lax.all_to_all(sent, LAT, split_axis=0, concat_axis=0, tiled=True)
    slot = ma_place * slots + jnp.minimum(lat_place, slots - 1)
    wave = lax.dynamic_slice_in_dim(pair_wave, slot, 1)
    got = pltpu.with_memory_space_constraint(got.reshape(-1, LANES), pltpu.VMEM)
    parts = sums_call(wave, got, lat_count, lat_rows, coef_rows)
    parts = parts.astype(jnp.float16).reshape(lat_count * N_MA, 4, LANES)
    spectra = lax.all_to_all(parts, ALL, split_axis=0, concat_axis=0, tiled=True)
    spectra = spectra[: slots * N_MA].astype(jnp.float32)
    spectra = spectra * jnp.exp2(spectra[:, :, PART:][:, :, :1] - TOP)
    spectra = spectra[:, :, :PART]
    high, low = in_two(spectra)
    base_high, base_low = basis(pair_wave, slots)

    def times(h, b, parity):
        return lax.dot_general(
            h[:, 2 * parity : 2 * parity + 2],
            b[parity],
            (((1, 0), (0, 1)), ((), ())),
            preferred_element_type=jnp.float32,
        )

    halves = [
        times(high, base_high, k) + times(low, base_high, k) + times(high, base_low, k)
        for k in range(2)
    ]
    return jnp.concatenate([halves[0] + halves[1], halves[0] - halves[1]], axis=1)


def solution(mesh):
    split = Mesh(mesh.devices.reshape(8, mesh.shape["lat"] // 8, 4, 2), ALL)
    placed = (P(), P(MA, LAT, None), P(MA, LAT, None))
    return jax.shard_map(
        body, mesh=split, in_specs=placed, out_specs=P(ALL, None), check_vma=False
    )
```

time: 105 us -> 96.2 us (0.916)
  local copies, waits for them, and re-layouts: 13.5 us -> 2.3 us
  Pallas kernels: 0 us -> 4.95 us
  between operations: 3.71 us -> 0.16 us
  waiting for transfers between devices: 38.1 us -> 40.5 us
  matrix products: 3.44 us -> 2.06 us
    pallas_call x0 -> x2, Pallas kernels: none -> 4.95 us  [the longest x1 2.53 us: pack_call(): pl.pallas_call(pack_kernel, out_shape=jax.ShapeDtypeStruct((lat_count * c...]
    reshape x6 -> x0, local copies, waits for them, and re-layouts: 3.97 us -> none  [the longest x1 2.03 us: body(): sent = sent.reshape(lat_count, -1, 4, LANES)]
    all_to_all x1, waiting for transfers between devices: 27.3 us -> 29.9 us  [body(): got = lax.all_to_all(sent, LAT, split_axis=0, concat_axis=0, tiled=True)]
    unnamed x10 -> x6, local copies, waits for them, and re-layouts: 3.42 us -> 1.31 us
    mul x3 -> x0, local copies, waits for them, and re-layouts: 1.77 us -> none  [body(): parts = parts.reshape(lat_count, 4, N_MA, PART) * jnp.exp2(TOP - power)]
    dot_general x1 -> x0, matrix products: 1.37 us -> none  [body(): jnp.dot(weights, jnp.concatenate([even, odd], axis=1), preferred_element_...]
    concatenate x2 -> x0, local copies, waits for them, and re-layouts: 1.19 us -> none  [the longest x1 1.14 us: body(): parts = jnp.concatenate([parts, note], axis=2).astype(jnp.float16)]
  transfers between devices with their start and end apart: 2 -> 2, of which waited for: 2 -> 2; matrix products, arithmetic and copies ran while one was open for 12% -> 13% of each run, Pallas kernels for 0% -> 0%
where the time goes in v2:
time: 96.2 us; the launch traced here: 95.9 us
  waiting for transfers between devices  40.5 us (42%)
  starting transfers between devices  32.4 us (34%)
  other arithmetic  13.5 us (14%)
  Pallas kernels  4.95 us (5%)
  local copies, waits for them, and re-layouts  2.3 us (2%)
  matrix products  2.06 us (2%)
    all_to_all x1, waiting for transfers between devices, body(): got = lax.all_to_all(sent, LAT, split_axis=0, concat_axis=0, tiled=True)  29.9 us
    all_to_all x1, starting transfers between devices, body(): got = lax.all_to_all(sent, LAT, split_axis=0, concat_axis=0, tiled=True)  17.1 us
    all_to_all x1, starting transfers between devices, body(): lax.all_to_all(parts, ALL, split_axis=0, concat_axis=0, tiled=True)  15.3 us
    all_to_all x1, waiting for transfers between devices, body(): lax.all_to_all(parts, ALL, split_axis=0, concat_axis=0, tiled=True)  10.6 us
    mul x1, other arithmetic, basis(): weight * jnp.cos(radians)  9.39 us
    pallas_call x1, Pallas kernels, pack_call(): pl.pallas_call(pack_kernel, out_shape=jax.ShapeDtypeStruct((lat_count * c...  2.53 us
    pallas_call x1, Pallas kernels, sums_call(): pl.pallas_call(functools.partial(sums_kernel, lat_count=lat_count, lat_ro...  2.42 us
    convert_element_type x2, other arithmetic, in_two(): return (high.astype(jnp.bfloat16), (full - high).astype(jnp.bfloat16))  2.15 us
  transfers between devices with their start and end apart: 2, of which 2 were waited for; matrix products, arithmetic and copies ran while one was open for 13% of the time, Pallas kernels for 0%

profile of v2, /device:TPU:1, one launch (start us, length us, event | category | flops | bytes accessed | tf_op | source)
XLA Modules:
  0.0 95.9 jit_solution(16943853290935134462)
XLA Ops:
  0.0 0.0 copy-start.1
  0.0 2.5 %shard_map.37 = bf16[4864,128]{1,0:T(8,128)(2,1)} custom-call(bf16[10,45,768]{2,1,0:T(8,128)(2,1)} %bitcast.51, bf16[12,45,168]{2,1,0:T(8,128)(2,1)} %bitcast.52), custom_call_target="tpu_custom_call" | custom-call | tf_op jit(solution)/shard_map/pallas_call | solution.py:130
  2.5 17.1 %all-to-all-start = ((bf16[64,19,4,128]{3,2,1,0:T(4,128)(2,1)}), bf16[64,19,4,128]{3,2,1,0:T(4,128)(2,1)S(1)}, u32[]{:S(2)}, u32[]{:S(2)}) async-start(bf16[64,19,4,128]{3,2,1,0:T(4,128)(2,1)} %bitcast.50), calls=%async_computation | async-start | bytes 2490368 | tf_op jit(solution)/shard_map/all_to_all | solution.py:164
  19.7 0.0 copy-done.1
  19.7 0.1 reshape.198
  19.8 0.1 copy.8
  19.9 0.1 reshape.199
  20.0 0.6 dynamic_slice.3.wave_ref
  20.5 29.9 %all-to-all-done = bf16[64,19,4,128]{3,2,1,0:T(4,128)(2,1)S(1)} async-done(((bf16[64,19,4,128]{3,2,1,0:T(4,128)(2,1)}), bf16[64,19,4,128]{3,2,1,0:T(4,128)(2,1)S(1)}, u32[]{:S(2)}, u32[]{:S(2)}) %all-to-all-start) | async-done | bytes 1245216 | tf_op jit(solution)/shard_map/all_to_all | solution.py:164
  50.4 2.4 %shard_map.38 = f32[2048,128]{1,0:T(8,128)S(1)} custom-call(s32[1]{0:T(128)} %dynamic_slice.3.wave_ref, bf16[4864,128]{1,0:T(8,128)(2,1)S(1)} %bitcast.49), custom_call_target="tpu_custom_call" | custom-call | tf_op jit(solution)/shard_map/pallas_call | solution.py:87
  52.9 0.9 convert_element_type.32
  53.7 15.3 %all-to-all-start.1 = ((f16[512,4,128]{2,1,0:T(4,128)(2,1)}), f16[512,4,128]{2,1,0:T(4,128)(2,1)S(1)}, u32[]{:S(2)}, u32[]{:S(2)}) async-start(f16[512,4,128]{2,1,0:T(4,128)(2,1)} %bitcast.4), calls=%async_computation.1 | async-start | bytes 1048576 | tf_op jit(solution)/shard_map/all_to_all | solution.py:170
  69.1 9.4 %cosine_multiply_fusion = (f32[2,1,360,720]{3,2,1,0:T(8,128)S(1)}, f32[2,1,360,720]{3,2,1,0:T(8,128)S(1)}) fusion(s32[2,360]{1,0:T(2,128)S(1)} %pad_add_fusion, f32[2,360]{1,0:T(2,128)S(1)} %get-tuple-element.13, f32[2,360]{1,0:T(2,128)S(1)} %get-tuple-element.14), kind=kLoop, calls=%fused_computation.8 | loop fusion | flops 5702400 | bytes 4155840 | tf_op jit(solution)/shard_map/mul | solution.py:153
  78.5 2.1 %reduce-precision_convert_fusion = (bf16[2,2,360,720]{3,2,1,0:T(8,128)(2,1)S(1)}, bf16[2,2,360,720]{3,2,1,0:T(8,128)(2,1)}) fusion(f32[2,1,360,720]{3,2,1,0:T(8,128)S(1)} %get-tuple-element.12, f32[2,1,360,720]{3,2,1,0:T(8,128)S(1)} %get-tuple-element.11), kind=kLoop, calls=%fused_computation.1 | loop fusion | flops 5184000 | bytes 8294400 | tf_op jit(solution)/shard_map/convert_element_type | solution.py:141
  80.6 10.6 %all-to-all-done.1 = f16[512,4,128]{2,1,0:T(4,128)(2,1)S(1)} async-done(((f16[512,4,128]{2,1,0:T(4,128)(2,1)}), f16[512,4,128]{2,1,0:T(4,128)(2,1)S(1)}, u32[]{:S(2)}, u32[]{:S(2)}) %all-to-all-start.1) | async-done | bytes 524320 | tf_op jit(solution)/shard_map/all_to_all | solution.py:170
  91.2 0.1 slice.50
  91.3 0.4 copy.10
  91.8 0.1 convert_element_type.33
  91.9 0.1 reduce-precision_convert_fusion.1
  91.9 0.0 copy-start
  91.9 0.4 convolution_bitcast_fusion.4
  92.3 0.3 convolution_bitcast_fusion.1
  92.6 0.9 copy-done
  93.5 0.3 convolution_bitcast_fusion.3
  93.9 0.3 convolution_bitcast_fusion
  94.2 0.3 fusion.9
  94.6 0.3 fusion.17
  94.9 1.0 %pad_maximum_fusion.1 = f32[105,1440]{1,0:T(8,128)} fusion(f32[105,720]{1,0:T(8,128)S(1)} %get-tuple-element.10, f32[105,720]{1,0:T(8,128)S(1)} %get-tuple-element.9), kind=kLoop, calls=%fused_computation.31 | loop fusion | flops 151200 | bytes 1209600 | tf_op jit(solution)/shard_map/concatenate | solution.py:189
  (6 shorter events, 0.1 us)
Async XLA Ops:
  0.0 19.7 %copy-start.1 = (s32[360]{0:T(512)S(1)}, s32[360]{0:T(512)}, u32[]{:S(2)}) copy-start(s32[360]{0:T(512)} %param.3) | copy-start | bytes 4324
  2.5 47.9 %all-to-all-start = ((bf16[64,19,4,128]{3,2,1,0:T(4,128)(2,1)}), bf16[64,19,4,128]{3,2,1,0:T(4,128)(2,1)S(1)}, u32[]{:S(2)}, u32[]{:S(2)}) async-start(bf16[64,19,4,128]{3,2,1,0:T(4,128)(2,1)} %bitcast.50), calls=%async_computation | async-start | bytes 2490368 | tf_op jit(solution)/shard_map/all_to_all | solution.py:164
  53.7 37.5 %all-to-all-start.1 = ((f16[512,4,128]{2,1,0:T(4,128)(2,1)}), f16[512,4,128]{2,1,0:T(4,128)(2,1)S(1)}, u32[]{:S(2)}, u32[]{:S(2)}) async-start(f16[512,4,128]{2,1,0:T(4,128)(2,1)} %bitcast.4), calls=%async_computation.1 | async-start | bytes 1048576 | tf_op jit(solution)/shard_map/all_to_all | solution.py:170
  91.9 1.6 %copy-start = (bf16[2,2,360,720]{3,2,1,0:T(8,128)(2,1)S(1)}, bf16[2,2,360,720]{3,2,1,0:T(8,128)(2,1)}, u32[]{:S(2)}) copy-start(bf16[2,2,360,720]{3,2,1,0:T(8,128)(2,1)} %get-tuple-element.8) | copy-start | bytes 6220804

commit v3 on v2

--- a/solution.py
+++ b/solution.py
@@ -21,6 +21,8 @@
 MA = ("x", "core")
 ALL = ("y", "z", "x", "core")
 TOP = 14
+GRANT = 24 * 2**20
+FETCHES = 5
 
 
 def sums_kernel(wave_ref, got_ref, out_ref, wide_ref, weights_ref, real_ref, imag_ref, sums_ref, turned_ref, *, lat_count, lat_rows, coef_rows):
@@ -34,13 +36,14 @@
             weights_ref[i * lat_count : (i + 1) * lat_count, b * LANES : (b + 1) * LANES] = piece.astype(jnp.bfloat16)
     at = lat_rows * blocks
     tail = 2 * CH - LANES
+    split = LANES - CH
     lane = lax.broadcasted_iota(jnp.int32, (lat_count, LANES), 1)
     for k in range(coef_rows):
         main = wide_ref[pl.ds(at + k, lat_count, stride=chunk), :]
-        rest = wide_ref[pl.ds(at + coef_rows + k % 4, lat_count, stride=chunk), :]
-        split = LANES - CH
-        moved = pltpu.roll(main, LANES - CH, 1)
-        rest = pltpu.roll(rest, (split - tail * (k // 4)) % LANES, 1)
+        row, place = tail_place(k, lat_rows, coef_rows, blocks, tail)
+        rest = wide_ref[pl.ds(row, lat_count, stride=chunk), :]
+        moved = pltpu.roll(main, split, 1)
+        rest = pltpu.roll(rest, (split - place) % LANES, 1)
         imag = jnp.where(lane < split, moved, rest)
         real_ref[pl.ds(k, lat_count, stride=coef_rows), :] = jnp.where(lane < CH, main, 0.0)
         imag_ref[pl.ds(k, lat_count, stride=coef_rows), :] = jnp.where(lane < CH, imag, 0.0)
@@ -97,6 +100,7 @@
             vm((lat_count * lat_rows, 4 * LANES), jnp.float32),
             vm((lat_count * (4 * N_MA + 4), LANES), jnp.float32),
         ],
+        compiler_params=pltpu.CompilerParams(vmem_limit_bytes=GRANT),
     )(wave, got)
 
 
@@ -104,41 +108,132 @@
     lat_rows, slots, degree_rows = legendre_ref.shape
     coef_rows = coefs_ref.shape[0]
     blocks = degree_rows // LANES
-    chunk = lat_rows * blocks + coef_rows + 4
+    chunk = chunk_rows(lat_rows, coef_rows, blocks)
+    tail = 2 * CH - LANES
+    top = wide_ref.shape[0]
+    wide_ref[top - 16 :, :] = jnp.zeros((16, LANES), jnp.float32)
     for i in range(lat_rows):
         for b in range(blocks):
             piece = legendre_ref[i, :, b * LANES : (b + 1) * LANES].astype(jnp.float32)
+            if b == blocks - 1:
+                rest = coefs_ref[i, :, LANES:].astype(jnp.float32)
+                piece = jnp.concatenate([piece[:, : LANES - tail], rest], axis=1)
             wide_ref[pl.ds(i * blocks + b, slots, stride=chunk), :] = piece
     at = lat_rows * blocks
-    tail = 2 * CH - LANES
     for k in range(coef_rows):
-        wide_ref[pl.ds(at + k, slots, stride=chunk), :] = coefs_ref[k, :, :LANES].astype(jnp.float32)
-    for t in range(4):
-        parts = [coefs_ref[t + 4 * j, :, LANES:].astype(jnp.float32) for j in range(3)]
-        parts.append(jnp.zeros((slots, LANES - 3 * tail), jnp.float32))
-        wide_ref[pl.ds(at + coef_rows + t, slots, stride=chunk), :] = jnp.concatenate(parts, axis=1)
-    full = slots * chunk
-    out_ref[:full, :] = wide_ref[...].astype(jnp.bfloat16)
-    out_ref[full:, :] = jnp.zeros((out_ref.shape[0] - full, LANES), jnp.bfloat16)
+        piece = coefs_ref[k, :, :LANES].astype(jnp.float32)
+        wide_ref[pl.ds(at + k, slots, stride=chunk), :] = piece
+    last = [coefs_ref[k, :, LANES:].astype(jnp.float32) for k in range(lat_rows, coef_rows)]
+    last.append(jnp.zeros((slots, LANES - len(last) * tail), jnp.float32))
+    last = jnp.concatenate(last, axis=1)
+    for t in range(at + coef_rows, chunk):
+        wide_ref[pl.ds(t, slots, stride=chunk), :] = last
+    out_ref[:top, :] = wide_ref[...].astype(jnp.bfloat16)
+    out_ref[top:, :] = jnp.zeros((out_ref.shape[0] - top, LANES), jnp.bfloat16)
+
+
+def chunk_rows(lat_rows, coef_rows, blocks):
+    rows = lat_rows * blocks + coef_rows + 1
+    return rows + rows % 2
+
+
+def tail_place(k, lat_rows, coef_rows, blocks, tail):
+    if k < lat_rows:
+        return k * blocks + blocks - 1, LANES - tail
+    return lat_rows * blocks + coef_rows, (k - lat_rows) * tail
 
 
 def pack_call(legendre, coefs, lat_count):
     slots, lat_rows, degree_rows = legendre.shape
     coef_rows = coefs.shape[1]
-    chunk = lat_rows * degree_rows // LANES + coef_rows + 4
+    chunk = chunk_rows(lat_rows, coef_rows, degree_rows // LANES)
     vm = pltpu.VMEM
     return pl.pallas_call(
         pack_kernel,
         out_shape=jax.ShapeDtypeStruct((lat_count * chunk, LANES), jnp.bfloat16),
         in_specs=[pl.BlockSpec(memory_space=vm)] * 2,
         out_specs=pl.BlockSpec(memory_space=vm),
-        scratch_shapes=[vm((slots * chunk, LANES), jnp.float32)],
+        scratch_shapes=[vm((-(-slots * chunk // 16) * 16, LANES), jnp.float32)],
     )(jnp.transpose(legendre, (1, 0, 2)), jnp.transpose(coefs, (1, 0, 2)))
 
 
-def in_two(full):
-    high = lax.reduce_precision(full, 8, 7)
-    return high.astype(jnp.bfloat16), (full - high).astype(jnp.bfloat16)
+def synth_kernel(spectra_ref, high_ref, low_hbm, out_ref, low_ref, sems):
+    step = low_ref.shape[1] // FETCHES
+    fetches = []
+    for parity in range(2):
+        for k in range(FETCHES):
+            part = pl.ds(k * step, step)
+            fetches.append(
+                pltpu.make_async_copy(
+                    low_hbm.at[parity, part],
+                    low_ref.at[parity, part],
+                    sems.at[parity * FETCHES + k],
+                )
+            )
+            fetches[-1].start()
+    count = spectra_ref.shape[0] // 4
+    over_rows = (((0,), (0,)), ((), ()))
+    highs, sums = [], []
+    for parity in range(2):
+        rows = []
+        for e in range(2):
+            row = spectra_ref[pl.ds(2 * parity + e, count, stride=4), :]
+            rows.append(row * jnp.exp2(row[:, LANES - 1 :] - TOP))
+        row = jnp.concatenate(rows, axis=0)
+        high = row.astype(jnp.bfloat16)
+        low = (row - high.astype(jnp.float32)).astype(jnp.bfloat16)
+        both = lax.dot_general(
+            jnp.concatenate([high, low], axis=1),
+            high_ref[parity],
+            over_rows,
+            preferred_element_type=jnp.float32,
+        )
+        highs.append(high)
+        sums.append(both[:LANES] + both[LANES:])
+    for parity in range(2):
+        for k in range(FETCHES):
+            fetches[parity * FETCHES + k].wait()
+        more = lax.dot_general(
+            highs[parity], low_ref[parity], over_rows, preferred_element_type=jnp.float32
+        )
+        sums[parity] = (sums[parity] + more)[:PART]
+    out_ref[:, :HALF] = sums[0] + sums[1]
+    out_ref[:, HALF:] = sums[0] - sums[1]
+
+
+def synth_call(spectra, high, low):
+    vm = pltpu.VMEM
+    return pl.pallas_call(
+        synth_kernel,
+        out_shape=jax.ShapeDtypeStruct((PART, LON), jnp.float32),
+        in_specs=[pl.BlockSpec(memory_space=vm)] * 2 + [pl.BlockSpec(memory_space=pltpu.HBM)],
+        out_specs=pl.BlockSpec(memory_space=vm),
+        scratch_shapes=[vm(low.shape, low.dtype), pltpu.SemaphoreType.DMA((2 * FETCHES,))],
+        compiler_params=pltpu.CompilerParams(vmem_limit_bytes=GRANT),
+    )(spectra, high, low)
+
+
+def halve_kernel(full_ref, high_ref, low_ref):
+    full = full_ref[...]
+    high = full.astype(jnp.bfloat16)
+    high_ref[...] = high
+    low_ref[...] = (full - high.astype(jnp.float32)).astype(jnp.bfloat16)
+
+
+def halve_call(full):
+    parities, rows, columns = full.shape
+    block = pl.BlockSpec((None, rows, columns), lambda p: (p, 0, 0))
+    return pl.pallas_call(
+        halve_kernel,
+        grid=(parities,),
+        out_shape=[
+            pltpu.VMEM(full.shape, jnp.bfloat16),
+            pltpu.HBM(full.shape, jnp.bfloat16),
+        ],
+        in_specs=[block],
+        out_specs=[block] * 2,
+        compiler_params=pltpu.CompilerParams(vmem_limit_bytes=GRANT),
+    )(full)
 
 
 def basis(pair_wave, slots):
@@ -151,7 +246,7 @@
     radians = 2.0 * math.pi / LON * phase.astype(jnp.float32)
     weight = jnp.where(waves == 0, 1.0, 2.0).astype(jnp.float32)[:, :, None]
     full = jnp.stack([weight * jnp.cos(radians), -weight * jnp.sin(radians)], axis=1)
-    return in_two(full)
+    return full.reshape(2, -1, HALF)
 
 
 def body(pair_wave, legendre, coefs):
@@ -160,7 +255,7 @@
     ma_place = lax.axis_index(MA)
     slots, lat_rows = legendre.shape[:2]
     coef_rows = coefs.shape[1]
-    sent = pack_call(legendre, coefs, lat_count).reshape(lat_count, -1, 4, LANES)
+    sent = pack_call(legendre, coefs, lat_count).reshape(lat_count, -1, 2, LANES)
     got = lax.all_to_all(sent, LAT, split_axis=0, concat_axis=0, tiled=True)
     slot = ma_place * slots + jnp.minimum(lat_place, slots - 1)
     wave = lax.dynamic_slice_in_dim(pair_wave, slot, 1)
@@ -168,25 +263,12 @@
     parts = sums_call(wave, got, lat_count, lat_rows, coef_rows)
     parts = parts.astype(jnp.float16).reshape(lat_count * N_MA, 4, LANES)
     spectra = lax.all_to_all(parts, ALL, split_axis=0, concat_axis=0, tiled=True)
-    spectra = spectra[: slots * N_MA].astype(jnp.float32)
-    spectra = spectra * jnp.exp2(spectra[:, :, PART:][:, :, :1] - TOP)
-    spectra = spectra[:, :, :PART]
-    high, low = in_two(spectra)
-    base_high, base_low = basis(pair_wave, slots)
-
-    def times(h, b, parity):
-        return lax.dot_general(
-            h[:, 2 * parity : 2 * parity + 2],
-            b[parity],
-            (((1, 0), (0, 1)), ((), ())),
-            preferred_element_type=jnp.float32,
-        )
-
-    halves = [
-        times(high, base_high, k) + times(low, base_high, k) + times(high, base_low, k)
-        for k in range(2)
-    ]
-    return jnp.concatenate([halves[0] + halves[1], halves[0] - halves[1]], axis=1)
+    spectra = spectra[: slots * N_MA].astype(jnp.float32).reshape(-1, LANES)
+    high, low = halve_call(basis(pair_wave, slots))
+    high = pltpu.with_memory_space_constraint(high, pltpu.VMEM)
+    low = pltpu.with_memory_space_constraint(low, pltpu.HBM)
+    spectra = pltpu.with_memory_space_constraint(spectra, pltpu.VMEM)
+    return synth_call(spectra, high, low)
 
 
 def solution(mesh):

time: 96.2 us -> 94.8 us (0.985)
  Pallas kernels: 4.95 us -> 10.3 us
  other arithmetic: 13.5 us -> 10.8 us
  matrix products: 2.06 us -> 0 us
  local copies, waits for them, and re-layouts: 2.3 us -> 1 us
    pallas_call x0 -> x2, Pallas kernels: none -> 5.41 us  [the longest x1 3.79 us: synth_call(): pl.pallas_call(synth_kernel, out_shape=jax.ShapeDtypeStruct((PART, LON),...]
    convert_element_type x3 -> x0, other arithmetic: 2.2 us -> none  [the longest x2 2.15 us: in_two(): return (high.astype(jnp.bfloat16), (full - high).astype(jnp.bfloat16))]
    dot_general x6 -> x0, matrix products: 2.06 us -> none  [times(): lax.dot_general(h[:, 2 * parity:2 * parity + 2], b[parity], (((1, 0), (0,...]
    unnamed x6 -> x2, local copies, waits for them, and re-layouts: 1.31 us -> 0.01 us
    concatenate x1 -> x0, other arithmetic: 1.03 us -> none  [body(): jnp.concatenate([halves[0] + halves[1], halves[0] - halves[1]], axis=1)]
  transfers between devices with their start and end apart: 2 -> 2, of which waited for: 2 -> 2; matrix products, arithmetic and copies ran while one was open for 13% -> 11% of each run, Pallas kernels for 0% -> 2%
where the time goes in v3:
time: 94.8 us; the launch traced here: 94.6 us
  waiting for transfers between devices  40 us (42%)
  starting transfers between devices  32.2 us (34%)
  other arithmetic  10.8 us (11%)
  Pallas kernels  10.3 us (11%)
  local copies, waits for them, and re-layouts  1 us (1%)
    all_to_all x1, waiting for transfers between devices, body(): got = lax.all_to_all(sent, LAT, split_axis=0, concat_axis=0, tiled=True)  29.2 us
    all_to_all x1, starting transfers between devices, body(): got = lax.all_to_all(sent, LAT, split_axis=0, concat_axis=0, tiled=True)  17.1 us
    all_to_all x1, starting transfers between devices, body(): lax.all_to_all(parts, ALL, split_axis=0, concat_axis=0, tiled=True)  15 us
    all_to_all x1, waiting for transfers between devices, body(): lax.all_to_all(parts, ALL, split_axis=0, concat_axis=0, tiled=True)  10.9 us
    mul x1, other arithmetic, basis(): weight * jnp.cos(radians)  9.39 us
    pallas_call x1, Pallas kernels, synth_call(): pl.pallas_call(synth_kernel, out_shape=jax.ShapeDtypeStruct((PART, LON),...  3.79 us
    pallas_call x1, Pallas kernels, pack_call(): pl.pallas_call(pack_kernel, out_shape=jax.ShapeDtypeStruct((lat_count * c...  2.49 us
    pallas_call x1, Pallas kernels, sums_call(): pl.pallas_call(functools.partial(sums_kernel, lat_count=lat_count, lat_ro...  2.43 us
  transfers between devices with their start and end apart: 2, of which 2 were waited for; matrix products, arithmetic and copies ran while one was open for 11% of the time, Pallas kernels for 2%

profile of v3, /device:TPU:1, one launch (start us, length us, event | category | flops | bytes accessed | tf_op | source)
XLA Modules:
  0.0 94.6 jit_solution(4876958276278410302)
XLA Ops:
  0.0 0.0 copy-start
  0.0 2.5 %shard_map.37 = bf16[4736,128]{1,0:T(8,128)(2,1)} custom-call(bf16[10,45,768]{2,1,0:T(8,128)(2,1)} %bitcast.13, bf16[12,45,168]{2,1,0:T(8,128)(2,1)} %bitcast.14), custom_call_target="tpu_custom_call" | custom-call | tf_op jit(solution)/shard_map/pallas_call | solution.py:151
  2.5 17.1 %all-to-all-start = ((bf16[64,37,2,128]{3,2,1,0:T(2,128)(2,1)}), bf16[64,37,2,128]{3,2,1,0:T(2,128)(2,1)S(1)}, u32[]{:S(2)}, u32[]{:S(2)}) async-start(bf16[64,37,2,128]{3,2,1,0:T(2,128)(2,1)} %bitcast.11), calls=%async_computation | async-start | bytes 2424832 | tf_op jit(solution)/shard_map/all_to_all | solution.py:259
  19.6 0.0 copy-done
  19.6 0.1 reshape.208
  19.7 0.1 copy.4
  19.8 0.1 reshape.209
  19.9 0.6 dynamic_slice.3.wave_ref
  20.5 29.2 %all-to-all-done = bf16[64,37,2,128]{3,2,1,0:T(2,128)(2,1)S(1)} async-done(((bf16[64,37,2,128]{3,2,1,0:T(2,128)(2,1)}), bf16[64,37,2,128]{3,2,1,0:T(2,128)(2,1)S(1)}, u32[]{:S(2)}, u32[]{:S(2)}) %all-to-all-start) | async-done | bytes 1212448 | tf_op jit(solution)/shard_map/all_to_all | solution.py:259
  49.7 2.4 %shard_map.38 = f32[2048,128]{1,0:T(8,128)S(1)} custom-call(s32[1]{0:T(128)} %dynamic_slice.3.wave_ref, bf16[4736,128]{1,0:T(8,128)(2,1)S(1)} %bitcast.10), custom_call_target="tpu_custom_call" | custom-call | tf_op jit(solution)/shard_map/pallas_call | solution.py:90
  52.1 0.9 convert_element_type.18
  53.0 15.0 %all-to-all-start.1 = ((f16[512,4,128]{2,1,0:T(4,128)(2,1)}), f16[512,4,128]{2,1,0:T(4,128)(2,1)S(1)}, u32[]{:S(2)}, u32[]{:S(2)}) async-start(f16[512,4,128]{2,1,0:T(4,128)(2,1)} %bitcast.4), calls=%async_computation.1 | async-start | bytes 1048576 | tf_op jit(solution)/shard_map/all_to_all | solution.py:265
  68.1 9.4 %cosine_multiply_fusion = (f32[2,1,360,720]{3,2,1,0:T(8,128)S(1)}, f32[2,1,360,720]{3,2,1,0:T(8,128)S(1)}) fusion(s32[2,360]{1,0:T(2,128)S(1)} %pad_add_fusion, f32[2,360]{1,0:T(2,128)S(1)} %get-tuple-element.13, f32[2,360]{1,0:T(2,128)S(1)} %get-tuple-element.14), kind=kLoop, calls=%fused_computation.5 | loop fusion | flops 5702400 | bytes 4155840 | tf_op jit(solution)/shard_map/mul | solution.py:248
  77.5 0.4 pad_maximum_fusion
  77.9 1.6 %shard_map.39 = (bf16[2,720,720]{2,1,0:T(8,128)(2,1)S(1)}, bf16[2,720,720]{2,1,0:T(8,128)(2,1)}) custom-call(f32[2,720,720]{2,1,0:T(8,128)S(1)} %bitcast.9), custom_call_target="tpu_custom_call" | custom-call | tf_op jit(solution)/shard_map/pallas_call | solution.py:226
  79.5 10.9 %all-to-all-done.1 = f16[512,4,128]{2,1,0:T(4,128)(2,1)S(1)} async-done(((f16[512,4,128]{2,1,0:T(4,128)(2,1)}), f16[512,4,128]{2,1,0:T(4,128)(2,1)S(1)}, u32[]{:S(2)}, u32[]{:S(2)}) %all-to-all-start.1) | async-done | bytes 524320 | tf_op jit(solution)/shard_map/all_to_all | solution.py:265
  90.4 0.1 slice.4
  90.5 0.1 convert.1.spectra_ref
  90.6 3.8 %shard_map.40 = f32[105,1440]{1,0:T(8,128)} custom-call(f32[1440,128]{1,0:T(8,128)S(1)} %convert.1.spectra_ref, bf16[2,720,720]{2,1,0:T(8,128)(2,1)S(1)} %get-tuple-element.7.high_ref, bf16[2,720,720]{2,1,0:T(8,128)(2,1)} %get-tuple-element.8.low_hbm), custom_call_target="tpu_custom_call" | custom-call | tf_op jit(solution)/shard_map/pallas_call | solution.py:206
  (4 shorter events, 0.0 us)
Async XLA Ops:
  0.0 19.6 %copy-start = (s32[360]{0:T(512)S(1)}, s32[360]{0:T(512)}, u32[]{:S(2)}) copy-start(s32[360]{0:T(512)} %param.3) | copy-start | bytes 4324
  2.5 47.2 %all-to-all-start = ((bf16[64,37,2,128]{3,2,1,0:T(2,128)(2,1)}), bf16[64,37,2,128]{3,2,1,0:T(2,128)(2,1)S(1)}, u32[]{:S(2)}, u32[]{:S(2)}) async-start(bf16[64,37,2,128]{3,2,1,0:T(2,128)(2,1)} %bitcast.11), calls=%async_computation | async-start | bytes 2424832 | tf_op jit(solution)/shard_map/all_to_all | solution.py:259
  53.0 37.4 %all-to-all-start.1 = ((f16[512,4,128]{2,1,0:T(4,128)(2,1)}), f16[512,4,128]{2,1,0:T(4,128)(2,1)S(1)}, u32[]{:S(2)}, u32[]{:S(2)}) async-start(f16[512,4,128]{2,1,0:T(4,128)(2,1)} %bitcast.4), calls=%async_computation.1 | async-start | bytes 1048576 | tf_op jit(solution)/shard_map/all_to_all | solution.py:265

commit v4 on v3

--- a/solution.py
+++ b/solution.py
@@ -11,7 +11,7 @@
 
 DEG = 720
 LON = 1440
-HALF = LON // 2
+QUARTER = LON // 4
 CH = 84
 LAT_DEV = 10
 N_MA = 8
@@ -22,7 +22,6 @@
 ALL = ("y", "z", "x", "core")
 TOP = 14
 GRANT = 24 * 2**20
-FETCHES = 5
 
 
 def sums_kernel(wave_ref, got_ref, out_ref, wide_ref, weights_ref, real_ref, imag_ref, sums_ref, turned_ref, *, lat_count, lat_rows, coef_rows):
@@ -157,81 +156,71 @@
     )(jnp.transpose(legendre, (1, 0, 2)), jnp.transpose(coefs, (1, 0, 2)))
 
 
-def synth_kernel(spectra_ref, high_ref, low_hbm, out_ref, low_ref, sems):
-    step = low_ref.shape[1] // FETCHES
-    fetches = []
+def synth_kernel(spectra_ref, signs_ref, basis_ref, out_ref):
+    count = spectra_ref.shape[0] // 4
+    sums = []
     for parity in range(2):
-        for k in range(FETCHES):
-            part = pl.ds(k * step, step)
-            fetches.append(
-                pltpu.make_async_copy(
-                    low_hbm.at[parity, part],
-                    low_ref.at[parity, part],
-                    sems.at[parity * FETCHES + k],
-                )
+        sign = signs_ref[parity]
+        real, imag = (
+            row * jnp.exp2(row[:, LANES - 1 :] - TOP)
+            for row in (
+                spectra_ref[pl.ds(2 * parity + e, count, stride=4), :] for e in range(2)
             )
-            fetches[-1].start()
-    count = spectra_ref.shape[0] // 4
-    over_rows = (((0,), (0,)), ((), ()))
-    highs, sums = [], []
-    for parity in range(2):
-        rows = []
-        for e in range(2):
-            row = spectra_ref[pl.ds(2 * parity + e, count, stride=4), :]
-            rows.append(row * jnp.exp2(row[:, LANES - 1 :] - TOP))
-        row = jnp.concatenate(rows, axis=0)
+        )
+        if parity == 0:
+            later = [real * sign, imag * sign]
+        else:
+            later = [imag * -sign, real * sign]
+        row = jnp.concatenate(
+            [jnp.concatenate([real, imag], axis=0), jnp.concatenate(later, axis=0)], axis=1
+        )
         high = row.astype(jnp.bfloat16)
         low = (row - high.astype(jnp.float32)).astype(jnp.bfloat16)
-        both = lax.dot_general(
-            jnp.concatenate([high, low], axis=1),
-            high_ref[parity],
-            over_rows,
-            preferred_element_type=jnp.float32,
-        )
-        highs.append(high)
-        sums.append(both[:LANES] + both[LANES:])
-    for parity in range(2):
-        for k in range(FETCHES):
-            fetches[parity * FETCHES + k].wait()
-        more = lax.dot_general(
-            highs[parity], low_ref[parity], over_rows, preferred_element_type=jnp.float32
-        )
-        sums[parity] = (sums[parity] + more)[:PART]
-    out_ref[:, :HALF] = sums[0] + sums[1]
-    out_ref[:, HALF:] = sums[0] - sums[1]
-
-
-def synth_call(spectra, high, low):
+        both = over_rows(jnp.concatenate([high, low], axis=1), basis_ref[parity, 0])
+        more = over_rows(high, basis_ref[parity, 1])
+        sums.append(both[: 2 * LANES] + both[2 * LANES :] + more)
+    quarter = LON // 4
+    for turn in range(4):
+        at = turn % 2 * LANES
+        even = sums[0][at : at + PART]
+        odd = sums[1][at : at + PART]
+        cols = slice(turn * quarter, (turn + 1) * quarter)
+        out_ref[:, cols] = even + odd if turn < 2 else even - odd
+
+
+def over_rows(left, right):
+    return lax.dot_general(
+        left, right, (((0,), (0,)), ((), ())), preferred_element_type=jnp.float32
+    )
+
+
+def synth_call(spectra, signs, waves):
     vm = pltpu.VMEM
     return pl.pallas_call(
         synth_kernel,
         out_shape=jax.ShapeDtypeStruct((PART, LON), jnp.float32),
-        in_specs=[pl.BlockSpec(memory_space=vm)] * 2 + [pl.BlockSpec(memory_space=pltpu.HBM)],
+        in_specs=[pl.BlockSpec(memory_space=vm)] * 3,
         out_specs=pl.BlockSpec(memory_space=vm),
-        scratch_shapes=[vm(low.shape, low.dtype), pltpu.SemaphoreType.DMA((2 * FETCHES,))],
         compiler_params=pltpu.CompilerParams(vmem_limit_bytes=GRANT),
-    )(spectra, high, low)
-
-
-def halve_kernel(full_ref, high_ref, low_ref):
+    )(spectra, signs, waves)
+
+
+def halve_kernel(full_ref, both_ref):
     full = full_ref[...]
     high = full.astype(jnp.bfloat16)
-    high_ref[...] = high
-    low_ref[...] = (full - high.astype(jnp.float32)).astype(jnp.bfloat16)
+    both_ref[0] = high
+    both_ref[1] = (full - high.astype(jnp.float32)).astype(jnp.bfloat16)
 
 
 def halve_call(full):
     parities, rows, columns = full.shape
-    block = pl.BlockSpec((None, rows, columns), lambda p: (p, 0, 0))
+    vm = pltpu.VMEM
     return pl.pallas_call(
         halve_kernel,
         grid=(parities,),
-        out_shape=[
-            pltpu.VMEM(full.shape, jnp.bfloat16),
-            pltpu.HBM(full.shape, jnp.bfloat16),
-        ],
-        in_specs=[block],
-        out_specs=[block] * 2,
+        out_shape=vm((parities, 2, rows, columns), jnp.bfloat16),
+        in_specs=[pl.BlockSpec((None, rows, columns), lambda p: (p, 0, 0))],
+        out_specs=pl.BlockSpec((None, 2, rows, columns), lambda p: (p, 0, 0, 0)),
         compiler_params=pltpu.CompilerParams(vmem_limit_bytes=GRANT),
     )(full)
 
@@ -241,12 +230,13 @@
     other = DEG - 1 - first
     is_even = first % 2 == 0
     waves = jnp.stack([jnp.where(is_even, first, other), jnp.where(is_even, other, first)])
-    positions = jnp.arange(HALF, dtype=jnp.int32)
+    positions = jnp.arange(QUARTER, dtype=jnp.int32)
     phase = waves[:, :, None] * positions[None, None, :] % LON
     radians = 2.0 * math.pi / LON * phase.astype(jnp.float32)
     weight = jnp.where(waves == 0, 1.0, 2.0).astype(jnp.float32)[:, :, None]
     full = jnp.stack([weight * jnp.cos(radians), -weight * jnp.sin(radians)], axis=1)
-    return full.reshape(2, -1, HALF)
+    signs = jnp.where(waves % 4 < 2, 1.0, -1.0).astype(jnp.float32)
+    return full.reshape(2, -1, QUARTER), signs[:, :, None]
 
 
 def body(pair_wave, legendre, coefs):
@@ -264,11 +254,10 @@
     parts = parts.astype(jnp.float16).reshape(lat_count * N_MA, 4, LANES)
     spectra = lax.all_to_all(parts, ALL, split_axis=0, concat_axis=0, tiled=True)
     spectra = spectra[: slots * N_MA].astype(jnp.float32).reshape(-1, LANES)
-    high, low = halve_call(basis(pair_wave, slots))
-    high = pltpu.with_memory_space_constraint(high, pltpu.VMEM)
-    low = pltpu.with_memory_space_constraint(low, pltpu.HBM)
+    full, signs = basis(pair_wave, slots)
+    waves = pltpu.with_memory_space_constraint(halve_call(full), pltpu.VMEM)
     spectra = pltpu.with_memory_space_constraint(spectra, pltpu.VMEM)
-    return synth_call(spectra, high, low)
+    return synth_call(spectra, signs, waves)
 
 
 def solution(mesh):

time: 94.8 us -> 93.6 us (0.987)
  waiting for transfers between devices: 40 us -> 45.7 us
  other arithmetic: 10.8 us -> 6.01 us
  Pallas kernels: 10.3 us -> 7.86 us
    all_to_all x1, waiting for transfers between devices: 10.9 us -> 16.5 us  [body(): lax.all_to_all(parts, ALL, split_axis=0, concat_axis=0, tiled=True)]
    mul x1, other arithmetic: 9.39 us -> 4.73 us  [basis(): weight * jnp.cos(radians)]
    pallas_call x1, Pallas kernels: 1.62 us -> 0.37 us  [halve_call(): pl.pallas_call(halve_kernel, grid=(parities,), out_shape=vm((parities, 2,...]
    pallas_call x1, Pallas kernels: 3.79 us -> 2.58 us  [synth_call(): pl.pallas_call(synth_kernel, out_shape=jax.ShapeDtypeStruct((PART, LON),...]
  transfers between devices with their start and end apart: 2 -> 2, of which waited for: 2 -> 2; matrix products, arithmetic and copies ran while one was open for 11% -> 7% of each run, Pallas kernels for 2% -> 0%
where the time goes in v4:
time: 93.6 us; the launch traced here: 93.3 us
  waiting for transfers between devices  45.7 us (49%)
  starting transfers between devices  32.3 us (35%)
  Pallas kernels  7.86 us (8%)
  other arithmetic  6.01 us (6%)
  local copies, waits for them, and re-layouts  1.28 us (1%)
    all_to_all x1, waiting for transfers between devices, body(): got = lax.all_to_all(sent, LAT, split_axis=0, concat_axis=0, tiled=True)  29.2 us
    all_to_all x1, starting transfers between devices, body(): got = lax.all_to_all(sent, LAT, split_axis=0, concat_axis=0, tiled=True)  17.3 us
    all_to_all x1, waiting for transfers between devices, body(): lax.all_to_all(parts, ALL, split_axis=0, concat_axis=0, tiled=True)  16.5 us
    all_to_all x1, starting transfers between devices, body(): lax.all_to_all(parts, ALL, split_axis=0, concat_axis=0, tiled=True)  15 us
    mul x1, other arithmetic, basis(): weight * jnp.cos(radians)  4.73 us
    pallas_call x1, Pallas kernels, synth_call(): pl.pallas_call(synth_kernel, out_shape=jax.ShapeDtypeStruct((PART, LON),...  2.58 us
    pallas_call x1, Pallas kernels, pack_call(): pl.pallas_call(pack_kernel, out_shape=jax.ShapeDtypeStruct((lat_count * c...  2.48 us
    pallas_call x1, Pallas kernels, sums_call(): pl.pallas_call(functools.partial(sums_kernel, lat_count=lat_count, lat_ro...  2.43 us
  transfers between devices with their start and end apart: 2, of which 2 were waited for; matrix products, arithmetic and copies ran while one was open for 7% of the time, Pallas kernels for 0%

profile of v4, /device:TPU:1, one launch (start us, length us, event | category | flops | bytes accessed | tf_op | source)
XLA Modules:
  0.0 93.3 jit_solution(4601855406227731269)
XLA Ops:
  0.0 2.5 %shard_map.37 = bf16[4736,128]{1,0:T(8,128)(2,1)} custom-call(bf16[10,45,768]{2,1,0:T(8,128)(2,1)} %bitcast.15, bf16[12,45,168]{2,1,0:T(8,128)(2,1)} %bitcast.16), custom_call_target="tpu_custom_call" | custom-call | tf_op jit(solution)/shard_map/pallas_call | solution.py:150
  2.5 0.0 copy-start
  2.5 17.3 %all-to-all-start = ((bf16[64,37,2,128]{3,2,1,0:T(2,128)(2,1)}), bf16[64,37,2,128]{3,2,1,0:T(2,128)(2,1)S(1)}, u32[]{:S(2)}, u32[]{:S(2)}) async-start(bf16[64,37,2,128]{3,2,1,0:T(2,128)(2,1)} %bitcast.13), calls=%async_computation | async-start | bytes 2424832 | tf_op jit(solution)/shard_map/all_to_all | solution.py:249
  19.7 0.0 copy-done
  19.8 0.1 reshape.395
  19.8 0.1 copy.15
  19.9 0.1 reshape.396
  20.0 0.6 dynamic_slice.3.wave_ref
  20.6 29.2 %all-to-all-done = bf16[64,37,2,128]{3,2,1,0:T(2,128)(2,1)S(1)} async-done(((bf16[64,37,2,128]{3,2,1,0:T(2,128)(2,1)}), bf16[64,37,2,128]{3,2,1,0:T(2,128)(2,1)S(1)}, u32[]{:S(2)}, u32[]{:S(2)}) %all-to-all-start) | async-done | bytes 1212448 | tf_op jit(solution)/shard_map/all_to_all | solution.py:249
  49.8 2.4 %shard_map.38 = f32[2048,128]{1,0:T(8,128)S(1)} custom-call(s32[1]{0:T(128)} %dynamic_slice.3.wave_ref, bf16[4736,128]{1,0:T(8,128)(2,1)S(1)} %bitcast.12), custom_call_target="tpu_custom_call" | custom-call | tf_op jit(solution)/shard_map/pallas_call | solution.py:89
  52.2 0.9 convert_element_type.18
  53.1 15.0 %all-to-all-start.1 = ((f16[512,4,128]{2,1,0:T(4,128)(2,1)}), f16[512,4,128]{2,1,0:T(4,128)(2,1)S(1)}, u32[]{:S(2)}, u32[]{:S(2)}) async-start(f16[512,4,128]{2,1,0:T(4,128)(2,1)} %bitcast.4), calls=%async_computation.1 | async-start | bytes 1048576 | tf_op jit(solution)/shard_map/all_to_all | solution.py:255
  68.2 4.7 %cosine_multiply_fusion = (f32[2,1,360,360]{3,2,1,0:T(8,128)S(1)}, f32[2,1,360,360]{3,2,1,0:T(8,128)S(1)}) fusion(s32[2,360]{1,0:T(2,128)S(1)} %pad_add_fusion, f32[2,360]{1,0:T(2,128)S(1)} %get-tuple-element.9, f32[2,360]{1,0:T(2,128)S(1)} %get-tuple-element.10), kind=kLoop, calls=%fused_computation.5 | loop fusion | flops 2851200 | bytes 2082240 | tf_op jit(solution)/shard_map/mul | solution.py:237
  73.0 0.1 pad_maximum_fusion
  73.1 0.4 shard_map.39.basis_ref
  73.5 0.1 copy.17
  73.6 0.1 copy.16
  73.8 0.2 fusion.7.signs_ref
  74.0 16.5 %all-to-all-done.1 = f16[512,4,128]{2,1,0:T(4,128)(2,1)S(1)} async-done(((f16[512,4,128]{2,1,0:T(4,128)(2,1)}), f16[512,4,128]{2,1,0:T(4,128)(2,1)S(1)}, u32[]{:S(2)}, u32[]{:S(2)}) %all-to-all-start.1) | async-done | bytes 524320 | tf_op jit(solution)/shard_map/all_to_all | solution.py:255
  90.5 0.1 slice.4
  90.7 0.1 convert.1.spectra_ref
  90.7 2.6 %shard_map.40 = f32[105,1440]{1,0:T(8,128)} custom-call(f32[1440,128]{1,0:T(8,128)S(1)} %convert.1.spectra_ref, f32[2,360,1]{2,1,0:T(8,128)S(1)} %fusion.7.signs_ref, bf16[2,2,720,360]{3,2,1,0:T(8,128)(2,1)S(1)} %shard_map.39.basis_ref), custom_call_target="tpu_custom_call" | custom-call | tf_op jit(solution)/shard_map/pallas_call | solution.py:199
  (4 shorter events, 0.0 us)
Async XLA Ops:
  2.5 17.3 %copy-start = (s32[360]{0:T(512)S(1)}, s32[360]{0:T(512)}, u32[]{:S(2)}) copy-start(s32[360]{0:T(512)} %param.3) | copy-start | bytes 4324
  2.5 47.3 %all-to-all-start = ((bf16[64,37,2,128]{3,2,1,0:T(2,128)(2,1)}), bf16[64,37,2,128]{3,2,1,0:T(2,128)(2,1)S(1)}, u32[]{:S(2)}, u32[]{:S(2)}) async-start(bf16[64,37,2,128]{3,2,1,0:T(2,128)(2,1)} %bitcast.13), calls=%async_computation | async-start | bytes 2424832 | tf_op jit(solution)/shard_map/all_to_all | solution.py:249
  53.1 37.4 %all-to-all-start.1 = ((f16[512,4,128]{2,1,0:T(4,128)(2,1)}), f16[512,4,128]{2,1,0:T(4,128)(2,1)S(1)}, u32[]{:S(2)}, u32[]{:S(2)}) async-start(f16[512,4,128]{2,1,0:T(4,128)(2,1)} %bitcast.4), calls=%async_computation.1 | async-start | bytes 1048576 | tf_op jit(solution)/shard_map/all_to_all | solution.py:255

commit v5 on v4

--- a/solution.py
+++ b/solution.py
@@ -24,7 +24,31 @@
 GRANT = 24 * 2**20
 
 
-def sums_kernel(wave_ref, got_ref, out_ref, wide_ref, weights_ref, real_ref, imag_ref, sums_ref, turned_ref, *, lat_count, lat_rows, coef_rows):
+def sums_kernel(wave_ref, got_ref, out_ref, *scratch, **sizes):
+    @pl.when(wave_ref[0] >= 0)
+    def _():
+        slot_sums(wave_ref[0], got_ref, out_ref, *scratch, **sizes)
+
+    @pl.when(wave_ref[0] < 0)
+    def _():
+        out_ref[...] = jnp.zeros_like(out_ref)
+
+
+def slot_sums(
+    wave,
+    got_ref,
+    out_ref,
+    wide_ref,
+    weights_ref,
+    real_ref,
+    imag_ref,
+    sums_ref,
+    turned_ref,
+    *,
+    lat_count,
+    lat_rows,
+    coef_rows,
+):
     chunk = got_ref.shape[0] // lat_count
     blocks = DEG // LANES + 1
     depth = lat_count * coef_rows
@@ -46,7 +70,6 @@
         imag = jnp.where(lane < split, moved, rest)
         real_ref[pl.ds(k, lat_count, stride=coef_rows), :] = jnp.where(lane < CH, main, 0.0)
         imag_ref[pl.ds(k, lat_count, stride=coef_rows), :] = jnp.where(lane < CH, imag, 0.0)
-    wave = wave_ref[0]
     row = lax.broadcasted_iota(jnp.int32, (depth, 2 * LANES), 0)
     inside = row < DEG - wave
     outside = jnp.logical_and(row >= DEG - wave, row <= DEG)
@@ -249,6 +272,7 @@
     got = lax.all_to_all(sent, LAT, split_axis=0, concat_axis=0, tiled=True)
     slot = ma_place * slots + jnp.minimum(lat_place, slots - 1)
     wave = lax.dynamic_slice_in_dim(pair_wave, slot, 1)
+    wave = jnp.where(lat_place < slots, wave, -1)
     got = pltpu.with_memory_space_constraint(got.reshape(-1, LANES), pltpu.VMEM)
     parts = sums_call(wave, got, lat_count, lat_rows, coef_rows)
     parts = parts.astype(jnp.float16).reshape(lat_count * N_MA, 4, LANES)

time: 93.6 us -> 92.9 us (level)
  no operation moved by 1% of the time
where the time goes in v5:
time: 92.9 us; the launch traced here: 92.7 us
  waiting for transfers between devices  45 us (48%)
  starting transfers between devices  32.3 us (35%)
  Pallas kernels  7.22 us (8%)
  other arithmetic  6 us (6%)
  local copies, waits for them, and re-layouts  1.34 us (1%)
    all_to_all x1, waiting for transfers between devices, body(): got = lax.all_to_all(sent, LAT, split_axis=0, concat_axis=0, tiled=True)  28.4 us
    all_to_all x1, starting transfers between devices, body(): got = lax.all_to_all(sent, LAT, split_axis=0, concat_axis=0, tiled=True)  17.3 us
    all_to_all x1, waiting for transfers between devices, body(): lax.all_to_all(parts, ALL, split_axis=0, concat_axis=0, tiled=True)  16.5 us
    all_to_all x1, starting transfers between devices, body(): lax.all_to_all(parts, ALL, split_axis=0, concat_axis=0, tiled=True)  15 us
    mul x1, other arithmetic, basis(): weight * jnp.cos(radians)  4.73 us
    pallas_call x1, Pallas kernels, synth_call(): pl.pallas_call(synth_kernel, out_shape=jax.ShapeDtypeStruct((PART, LON),...  2.58 us
    pallas_call x1, Pallas kernels, pack_call(): pl.pallas_call(pack_kernel, out_shape=jax.ShapeDtypeStruct((lat_count * c...  2.48 us
  transfers between devices with their start and end apart: 2, of which 2 were waited for; matrix products, arithmetic and copies ran while one was open for 7% of the time, Pallas kernels for 0%

profile of v5, /device:TPU:1, one launch (start us, length us, event | category | flops | bytes accessed | tf_op | source)
XLA Modules:
  0.0 92.7 jit_solution(696485475913559298)
XLA Ops:
  0.0 2.5 %shard_map.37 = bf16[4736,128]{1,0:T(8,128)(2,1)} custom-call(bf16[10,45,768]{2,1,0:T(8,128)(2,1)} %bitcast.16, bf16[12,45,168]{2,1,0:T(8,128)(2,1)} %bitcast.17), custom_call_target="tpu_custom_call" | custom-call | tf_op jit(solution)/shard_map/pallas_call | solution.py:173
  2.5 0.0 copy-start
  2.5 17.3 %all-to-all-start = ((bf16[64,37,2,128]{3,2,1,0:T(2,128)(2,1)}), bf16[64,37,2,128]{3,2,1,0:T(2,128)(2,1)S(1)}, u32[]{:S(2)}, u32[]{:S(2)}) async-start(bf16[64,37,2,128]{3,2,1,0:T(2,128)(2,1)} %bitcast.14), calls=%async_computation | async-start | bytes 2424832 | tf_op jit(solution)/shard_map/all_to_all | solution.py:272
  19.7 0.0 copy-done
  19.8 0.1 reshape.396
  19.8 0.1 copy.15
  19.9 0.1 reshape.397
  20.0 0.7 dynamic_slice.3
  21.4 28.4 %all-to-all-done = bf16[64,37,2,128]{3,2,1,0:T(2,128)(2,1)S(1)} async-done(((bf16[64,37,2,128]{3,2,1,0:T(2,128)(2,1)}), bf16[64,37,2,128]{3,2,1,0:T(2,128)(2,1)S(1)}, u32[]{:S(2)}, u32[]{:S(2)}) %all-to-all-start) | async-done | bytes 1212448 | tf_op jit(solution)/shard_map/all_to_all | solution.py:272
  49.8 1.8 %shard_map.38 = f32[2048,128]{1,0:T(8,128)S(1)} custom-call(s32[1]{0:T(128)S(6)} %select_n.155.wave_ref, bf16[4736,128]{1,0:T(8,128)(2,1)S(1)} %bitcast.13), custom_call_target="tpu_custom_call" | custom-call | tf_op jit(solution)/shard_map/pallas_call | solution.py:112
  51.6 0.9 convert_element_type.18
  52.5 15.0 %all-to-all-start.1 = ((f16[512,4,128]{2,1,0:T(4,128)(2,1)}), f16[512,4,128]{2,1,0:T(4,128)(2,1)S(1)}, u32[]{:S(2)}, u32[]{:S(2)}) async-start(f16[512,4,128]{2,1,0:T(4,128)(2,1)} %bitcast.5), calls=%async_computation.1 | async-start | bytes 1048576 | tf_op jit(solution)/shard_map/all_to_all | solution.py:279
  67.6 4.7 %cosine_multiply_fusion = (f32[2,1,360,360]{3,2,1,0:T(8,128)S(1)}, f32[2,1,360,360]{3,2,1,0:T(8,128)S(1)}) fusion(s32[2,360]{1,0:T(2,128)S(1)} %pad_add_fusion, f32[2,360]{1,0:T(2,128)S(1)} %get-tuple-element.9, f32[2,360]{1,0:T(2,128)S(1)} %get-tuple-element.10), kind=kLoop, calls=%fused_computation.5 | loop fusion | flops 2851200 | bytes 2082240 | tf_op jit(solution)/shard_map/mul | solution.py:260
  72.3 0.1 pad_maximum_fusion
  72.5 0.4 shard_map.39.basis_ref
  72.8 0.1 copy.17
  73.0 0.1 copy.16
  73.1 0.2 fusion.7.signs_ref
  73.3 16.5 %all-to-all-done.1 = f16[512,4,128]{2,1,0:T(4,128)(2,1)S(1)} async-done(((f16[512,4,128]{2,1,0:T(4,128)(2,1)}), f16[512,4,128]{2,1,0:T(4,128)(2,1)S(1)}, u32[]{:S(2)}, u32[]{:S(2)}) %all-to-all-start.1) | async-done | bytes 524320 | tf_op jit(solution)/shard_map/all_to_all | solution.py:279
  89.9 0.1 slice.4
  90.0 0.1 convert.1.spectra_ref
  90.1 2.6 %shard_map.40 = f32[105,1440]{1,0:T(8,128)} custom-call(f32[1440,128]{1,0:T(8,128)S(1)} %convert.1.spectra_ref, f32[2,360,1]{2,1,0:T(8,128)S(1)} %fusion.7.signs_ref, bf16[2,2,720,360]{3,2,1,0:T(8,128)(2,1)S(1)} %shard_map.39.basis_ref), custom_call_target="tpu_custom_call" | custom-call | tf_op jit(solution)/shard_map/pallas_call | solution.py:222
  (4 shorter events, 0.0 us)
Async XLA Ops:
  2.5 17.3 %copy-start = (s32[360]{0:T(512)S(1)}, s32[360]{0:T(512)}, u32[]{:S(2)}) copy-start(s32[360]{0:T(512)} %param.3) | copy-start | bytes 4324
  2.5 47.3 %all-to-all-start = ((bf16[64,37,2,128]{3,2,1,0:T(2,128)(2,1)}), bf16[64,37,2,128]{3,2,1,0:T(2,128)(2,1)S(1)}, u32[]{:S(2)}, u32[]{:S(2)}) async-start(bf16[64,37,2,128]{3,2,1,0:T(2,128)(2,1)} %bitcast.14), calls=%async_computation | async-start | bytes 2424832 | tf_op jit(solution)/shard_map/all_to_all | solution.py:272
  52.5 37.4 %all-to-all-start.1 = ((f16[512,4,128]{2,1,0:T(4,128)(2,1)}), f16[512,4,128]{2,1,0:T(4,128)(2,1)S(1)}, u32[]{:S(2)}, u32[]{:S(2)}) async-start(f16[512,4,128]{2,1,0:T(4,128)(2,1)} %bitcast.5), calls=%async_computation.1 | async-start | bytes 1048576 | tf_op jit(solution)/shard_map/all_to_all | solution.py:279

commit v6 on v5

--- a/solution.py
+++ b/solution.py
@@ -39,7 +39,6 @@
     got_ref,
     out_ref,
     wide_ref,
-    weights_ref,
     real_ref,
     imag_ref,
     sums_ref,
@@ -53,10 +52,6 @@
     blocks = DEG // LANES + 1
     depth = lat_count * coef_rows
     wide_ref[...] = got_ref[...].astype(jnp.float32)
-    for i in range(lat_rows):
-        for b in range(blocks):
-            piece = wide_ref[pl.ds(i * blocks + b, lat_count, stride=chunk), :]
-            weights_ref[i * lat_count : (i + 1) * lat_count, b * LANES : (b + 1) * LANES] = piece.astype(jnp.bfloat16)
     at = lat_rows * blocks
     tail = 2 * CH - LANES
     split = LANES - CH
@@ -79,12 +74,29 @@
     second = jnp.where(outside, both, 0.0)
     even = jnp.where(is_even, first, second).astype(jnp.bfloat16)
     odd = jnp.where(is_even, second, first).astype(jnp.bfloat16)
-    weights = weights_ref[...]
-    even = jnp.dot(weights, even, preferred_element_type=jnp.float32)
-    odd = jnp.dot(weights, odd, preferred_element_type=jnp.float32)
-    sums_ref[:, : 2 * LANES] = even
-    sums_ref[:, 2 * LANES :] = odd
-    largest = jnp.maximum(jnp.max(jnp.abs(even)), jnp.max(jnp.abs(odd)))
+    right = jnp.concatenate([even, odd], axis=1)
+    largest = jnp.zeros((lat_count, 4 * LANES), jnp.float32)
+    for i in range(0, lat_rows, 2):
+        rows = slice(i * lat_count, (i + 2) * lat_count)
+        pieces = [
+            jnp.concatenate(
+                [
+                    wide_ref[pl.ds(n * blocks + b, lat_count, stride=chunk), :].astype(
+                        jnp.bfloat16
+                    )
+                    for b in range(blocks)
+                ],
+                axis=1,
+            )
+            for n in (i, i + 1)
+        ]
+        part = jnp.dot(
+            jnp.concatenate(pieces, axis=0), right, preferred_element_type=jnp.float32
+        )
+        sums_ref[rows, :] = part
+        part = jnp.abs(part)
+        largest = jnp.maximum(largest, jnp.maximum(part[:lat_count], part[lat_count:]))
+    largest = jnp.max(largest)
     largest = jnp.maximum(jnp.full((lat_count, LANES), largest, jnp.float32), 1e-30)
     power = jnp.clip(jnp.floor(jnp.log2(largest)), -100.0, 100.0)
     scale = jnp.exp2(TOP - power)
@@ -116,7 +128,6 @@
         out_specs=pl.BlockSpec(memory_space=vm),
         scratch_shapes=[
             vm(got.shape, jnp.float32),
-            vm((lat_count * lat_rows, blocks * LANES), jnp.bfloat16),
             vm((lat_count * coef_rows, LANES), jnp.float32),
             vm((lat_count * coef_rows, LANES), jnp.float32),
             vm((lat_count * lat_rows, 4 * LANES), jnp.float32),

time: 92.9 us -> 92.7 us (level)
  no operation moved by 1% of the time
where the time goes in v6:
time: 92.7 us; the launch traced here: 92.4 us
  waiting for transfers between devices  45 us (49%)
  starting transfers between devices  32.3 us (35%)
  Pallas kernels  7 us (8%)
  other arithmetic  6 us (6%)
  local copies, waits for them, and re-layouts  1.34 us (1%)
    all_to_all x1, waiting for transfers between devices, body(): got = lax.all_to_all(sent, LAT, split_axis=0, concat_axis=0, tiled=True)  28.4 us
    all_to_all x1, starting transfers between devices, body(): got = lax.all_to_all(sent, LAT, split_axis=0, concat_axis=0, tiled=True)  17.3 us
    all_to_all x1, waiting for transfers between devices, body(): lax.all_to_all(parts, ALL, split_axis=0, concat_axis=0, tiled=True)  16.5 us
    all_to_all x1, starting transfers between devices, body(): lax.all_to_all(parts, ALL, split_axis=0, concat_axis=0, tiled=True)  15 us
    mul x1, other arithmetic, basis(): weight * jnp.cos(radians)  4.73 us
    pallas_call x1, Pallas kernels, synth_call(): pl.pallas_call(synth_kernel, out_shape=jax.ShapeDtypeStruct((PART, LON),...  2.58 us
    pallas_call x1, Pallas kernels, pack_call(): pl.pallas_call(pack_kernel, out_shape=jax.ShapeDtypeStruct((lat_count * c...  2.48 us
  transfers between devices with their start and end apart: 2, of which 2 were waited for; matrix products, arithmetic and copies ran while one was open for 7% of the time, Pallas kernels for 0%

profile of v6, /device:TPU:1, one launch (start us, length us, event | category | flops | bytes accessed | tf_op | source)
XLA Modules:
  0.0 92.4 jit_solution(8976331208279228081)
XLA Ops:
  0.0 2.5 %shard_map.37 = bf16[4736,128]{1,0:T(8,128)(2,1)} custom-call(bf16[10,45,768]{2,1,0:T(8,128)(2,1)} %bitcast.16, bf16[12,45,168]{2,1,0:T(8,128)(2,1)} %bitcast.17), custom_call_target="tpu_custom_call" | custom-call | tf_op jit(solution)/shard_map/pallas_call | solution.py:184
  2.5 0.0 copy-start
  2.5 17.3 %all-to-all-start = ((bf16[64,37,2,128]{3,2,1,0:T(2,128)(2,1)}), bf16[64,37,2,128]{3,2,1,0:T(2,128)(2,1)S(1)}, u32[]{:S(2)}, u32[]{:S(2)}) async-start(bf16[64,37,2,128]{3,2,1,0:T(2,128)(2,1)} %bitcast.14), calls=%async_computation | async-start | bytes 2424832 | tf_op jit(solution)/shard_map/all_to_all | solution.py:283
  19.7 0.0 copy-done
  19.8 0.1 reshape.396
  19.8 0.1 copy.15
  19.9 0.1 reshape.397
  20.0 0.7 dynamic_slice.3
  21.4 28.4 %all-to-all-done = bf16[64,37,2,128]{3,2,1,0:T(2,128)(2,1)S(1)} async-done(((bf16[64,37,2,128]{3,2,1,0:T(2,128)(2,1)}), bf16[64,37,2,128]{3,2,1,0:T(2,128)(2,1)S(1)}, u32[]{:S(2)}, u32[]{:S(2)}) %all-to-all-start) | async-done | bytes 1212448 | tf_op jit(solution)/shard_map/all_to_all | solution.py:283
  49.8 1.6 %shard_map.38 = f32[2048,128]{1,0:T(8,128)S(1)} custom-call(s32[1]{0:T(128)S(6)} %select_n.155.wave_ref, bf16[4736,128]{1,0:T(8,128)(2,1)S(1)} %bitcast.13), custom_call_target="tpu_custom_call" | custom-call | tf_op jit(solution)/shard_map/pallas_call | solution.py:124
  51.4 0.9 convert_element_type.18
  52.2 15.0 %all-to-all-start.1 = ((f16[512,4,128]{2,1,0:T(4,128)(2,1)}), f16[512,4,128]{2,1,0:T(4,128)(2,1)S(1)}, u32[]{:S(2)}, u32[]{:S(2)}) async-start(f16[512,4,128]{2,1,0:T(4,128)(2,1)} %bitcast.5), calls=%async_computation.1 | async-start | bytes 1048576 | tf_op jit(solution)/shard_map/all_to_all | solution.py:290
  67.4 4.7 %cosine_multiply_fusion = (f32[2,1,360,360]{3,2,1,0:T(8,128)S(1)}, f32[2,1,360,360]{3,2,1,0:T(8,128)S(1)}) fusion(s32[2,360]{1,0:T(2,128)S(1)} %pad_add_fusion, f32[2,360]{1,0:T(2,128)S(1)} %get-tuple-element.9, f32[2,360]{1,0:T(2,128)S(1)} %get-tuple-element.10), kind=kLoop, calls=%fused_computation.5 | loop fusion | flops 2851200 | bytes 2082240 | tf_op jit(solution)/shard_map/mul | solution.py:271
  72.1 0.1 pad_maximum_fusion
  72.3 0.4 shard_map.39.basis_ref
  72.6 0.1 copy.17
  72.8 0.1 copy.16
  72.9 0.2 fusion.7.signs_ref
  73.1 16.5 %all-to-all-done.1 = f16[512,4,128]{2,1,0:T(4,128)(2,1)S(1)} async-done(((f16[512,4,128]{2,1,0:T(4,128)(2,1)}), f16[512,4,128]{2,1,0:T(4,128)(2,1)S(1)}, u32[]{:S(2)}, u32[]{:S(2)}) %all-to-all-start.1) | async-done | bytes 524320 | tf_op jit(solution)/shard_map/all_to_all | solution.py:290
  89.7 0.1 slice.4
  89.8 0.1 convert.1.spectra_ref
  89.9 2.6 %shard_map.40 = f32[105,1440]{1,0:T(8,128)} custom-call(f32[1440,128]{1,0:T(8,128)S(1)} %convert.1.spectra_ref, f32[2,360,1]{2,1,0:T(8,128)S(1)} %fusion.7.signs_ref, bf16[2,2,720,360]{3,2,1,0:T(8,128)(2,1)S(1)} %shard_map.39.basis_ref), custom_call_target="tpu_custom_call" | custom-call | tf_op jit(solution)/shard_map/pallas_call | solution.py:233
  (4 shorter events, 0.0 us)
Async XLA Ops:
  2.5 17.3 %copy-start = (s32[360]{0:T(512)S(1)}, s32[360]{0:T(512)}, u32[]{:S(2)}) copy-start(s32[360]{0:T(512)} %param.3) | copy-start | bytes 4324
  2.5 47.3 %all-to-all-start = ((bf16[64,37,2,128]{3,2,1,0:T(2,128)(2,1)}), bf16[64,37,2,128]{3,2,1,0:T(2,128)(2,1)S(1)}, u32[]{:S(2)}, u32[]{:S(2)}) async-start(bf16[64,37,2,128]{3,2,1,0:T(2,128)(2,1)} %bitcast.14), calls=%async_computation | async-start | bytes 2424832 | tf_op jit(solution)/shard_map/all_to_all | solution.py:283
  52.2 37.4 %all-to-all-start.1 = ((f16[512,4,128]{2,1,0:T(4,128)(2,1)}), f16[512,4,128]{2,1,0:T(4,128)(2,1)S(1)}, u32[]{:S(2)}, u32[]{:S(2)}) async-start(f16[512,4,128]{2,1,0:T(4,128)(2,1)} %bitcast.5), calls=%async_computation.1 | async-start | bytes 1048576 | tf_op jit(solution)/shard_map/all_to_all | solution.py:290

commit v7 on v6

--- a/solution.py
+++ b/solution.py
@@ -143,8 +143,8 @@
     blocks = degree_rows // LANES
     chunk = chunk_rows(lat_rows, coef_rows, blocks)
     tail = 2 * CH - LANES
-    top = wide_ref.shape[0]
-    wide_ref[top - 16 :, :] = jnp.zeros((16, LANES), jnp.float32)
+    top = -(-slots * chunk // 16) * 16
+    wide_ref[top - 16 : top, :] = jnp.zeros((16, LANES), jnp.float32)
     for i in range(lat_rows):
         for b in range(blocks):
             piece = legendre_ref[i, :, b * LANES : (b + 1) * LANES].astype(jnp.float32)
@@ -161,7 +161,7 @@
     last = jnp.concatenate(last, axis=1)
     for t in range(at + coef_rows, chunk):
         wide_ref[pl.ds(t, slots, stride=chunk), :] = last
-    out_ref[:top, :] = wide_ref[...].astype(jnp.bfloat16)
+    out_ref[:top, :] = wide_ref[:top, :].astype(jnp.bfloat16)
     out_ref[top:, :] = jnp.zeros((out_ref.shape[0] - top, LANES), jnp.bfloat16)
 
 
@@ -186,7 +186,7 @@
         out_shape=jax.ShapeDtypeStruct((lat_count * chunk, LANES), jnp.bfloat16),
         in_specs=[pl.BlockSpec(memory_space=vm)] * 2,
         out_specs=pl.BlockSpec(memory_space=vm),
-        scratch_shapes=[vm((-(-slots * chunk // 16) * 16, LANES), jnp.float32)],
+        scratch_shapes=[vm((-(-slots // 8) * 8 * chunk, LANES), jnp.float32)],
     )(jnp.transpose(legendre, (1, 0, 2)), jnp.transpose(coefs, (1, 0, 2)))
 
 

time: 92.7 us -> 92.7 us (level)
  no operation moved by 1% of the time
where the time goes in v7:
time: 92.7 us; the launch traced here: 92.4 us
  waiting for transfers between devices  45 us (49%)
  starting transfers between devices  32.3 us (35%)
  Pallas kernels  7 us (8%)
  other arithmetic  6 us (6%)
  local copies, waits for them, and re-layouts  1.34 us (1%)
    all_to_all x1, waiting for transfers between devices, body(): got = lax.all_to_all(sent, LAT, split_axis=0, concat_axis=0, tiled=True)  28.4 us
    all_to_all x1, starting transfers between devices, body(): got = lax.all_to_all(sent, LAT, split_axis=0, concat_axis=0, tiled=True)  17.3 us
    all_to_all x1, waiting for transfers between devices, body(): lax.all_to_all(parts, ALL, split_axis=0, concat_axis=0, tiled=True)  16.5 us
    all_to_all x1, starting transfers between devices, body(): lax.all_to_all(parts, ALL, split_axis=0, concat_axis=0, tiled=True)  15 us
    mul x1, other arithmetic, basis(): weight * jnp.cos(radians)  4.73 us
    pallas_call x1, Pallas kernels, synth_call(): pl.pallas_call(synth_kernel, out_shape=jax.ShapeDtypeStruct((PART, LON),...  2.58 us
    pallas_call x1, Pallas kernels, pack_call(): pl.pallas_call(pack_kernel, out_shape=jax.ShapeDtypeStruct((lat_count * c...  2.48 us
  transfers between devices with their start and end apart: 2, of which 2 were waited for; matrix products, arithmetic and copies ran while one was open for 7% of the time, Pallas kernels for 0%

profile of v7, /device:TPU:1, one launch (start us, length us, event | category | flops | bytes accessed | tf_op | source)
XLA Modules:
  0.0 92.4 jit_solution(11857090345505723126)
XLA Ops:
  0.0 2.5 %shard_map.37 = bf16[4736,128]{1,0:T(8,128)(2,1)} custom-call(bf16[10,45,768]{2,1,0:T(8,128)(2,1)} %bitcast.16, bf16[12,45,168]{2,1,0:T(8,128)(2,1)} %bitcast.17), custom_call_target="tpu_custom_call" | custom-call | tf_op jit(solution)/shard_map/pallas_call | solution.py:184
  2.5 0.0 copy-start
  2.5 17.3 %all-to-all-start = ((bf16[64,37,2,128]{3,2,1,0:T(2,128)(2,1)}), bf16[64,37,2,128]{3,2,1,0:T(2,128)(2,1)S(1)}, u32[]{:S(2)}, u32[]{:S(2)}) async-start(bf16[64,37,2,128]{3,2,1,0:T(2,128)(2,1)} %bitcast.14), calls=%async_computation | async-start | bytes 2424832 | tf_op jit(solution)/shard_map/all_to_all | solution.py:283
  19.7 0.0 copy-done
  19.8 0.1 reshape.396
  19.8 0.1 copy.15
  19.9 0.1 reshape.397
  20.0 0.7 dynamic_slice.3
  21.4 28.4 %all-to-all-done = bf16[64,37,2,128]{3,2,1,0:T(2,128)(2,1)S(1)} async-done(((bf16[64,37,2,128]{3,2,1,0:T(2,128)(2,1)}), bf16[64,37,2,128]{3,2,1,0:T(2,128)(2,1)S(1)}, u32[]{:S(2)}, u32[]{:S(2)}) %all-to-all-start) | async-done | bytes 1212448 | tf_op jit(solution)/shard_map/all_to_all | solution.py:283
  49.8 1.6 %shard_map.38 = f32[2048,128]{1,0:T(8,128)S(1)} custom-call(s32[1]{0:T(128)S(6)} %select_n.155.wave_ref, bf16[4736,128]{1,0:T(8,128)(2,1)S(1)} %bitcast.13), custom_call_target="tpu_custom_call" | custom-call | tf_op jit(solution)/shard_map/pallas_call | solution.py:124
  51.4 0.9 convert_element_type.18
  52.2 15.0 %all-to-all-start.1 = ((f16[512,4,128]{2,1,0:T(4,128)(2,1)}), f16[512,4,128]{2,1,0:T(4,128)(2,1)S(1)}, u32[]{:S(2)}, u32[]{:S(2)}) async-start(f16[512,4,128]{2,1,0:T(4,128)(2,1)} %bitcast.5), calls=%async_computation.1 | async-start | bytes 1048576 | tf_op jit(solution)/shard_map/all_to_all | solution.py:290
  67.4 4.7 %cosine_multiply_fusion = (f32[2,1,360,360]{3,2,1,0:T(8,128)S(1)}, f32[2,1,360,360]{3,2,1,0:T(8,128)S(1)}) fusion(s32[2,360]{1,0:T(2,128)S(1)} %pad_add_fusion, f32[2,360]{1,0:T(2,128)S(1)} %get-tuple-element.9, f32[2,360]{1,0:T(2,128)S(1)} %get-tuple-element.10), kind=kLoop, calls=%fused_computation.5 | loop fusion | flops 2851200 | bytes 2082240 | tf_op jit(solution)/shard_map/mul | solution.py:271
  72.1 0.1 pad_maximum_fusion
  72.2 0.4 shard_map.39.basis_ref
  72.6 0.1 copy.17
  72.8 0.1 copy.16
  72.9 0.2 fusion.7.signs_ref
  73.1 16.5 %all-to-all-done.1 = f16[512,4,128]{2,1,0:T(4,128)(2,1)S(1)} async-done(((f16[512,4,128]{2,1,0:T(4,128)(2,1)}), f16[512,4,128]{2,1,0:T(4,128)(2,1)S(1)}, u32[]{:S(2)}, u32[]{:S(2)}) %all-to-all-start.1) | async-done | bytes 524320 | tf_op jit(solution)/shard_map/all_to_all | solution.py:290
  89.7 0.1 slice.4
  89.8 0.1 convert.1.spectra_ref
  89.9 2.6 %shard_map.40 = f32[105,1440]{1,0:T(8,128)} custom-call(f32[1440,128]{1,0:T(8,128)S(1)} %convert.1.spectra_ref, f32[2,360,1]{2,1,0:T(8,128)S(1)} %fusion.7.signs_ref, bf16[2,2,720,360]{3,2,1,0:T(8,128)(2,1)S(1)} %shard_map.39.basis_ref), custom_call_target="tpu_custom_call" | custom-call | tf_op jit(solution)/shard_map/pallas_call | solution.py:233
  (4 shorter events, 0.0 us)
Async XLA Ops:
  2.5 17.3 %copy-start = (s32[360]{0:T(512)S(1)}, s32[360]{0:T(512)}, u32[]{:S(2)}) copy-start(s32[360]{0:T(512)} %param.3) | copy-start | bytes 4324
  2.5 47.3 %all-to-all-start = ((bf16[64,37,2,128]{3,2,1,0:T(2,128)(2,1)}), bf16[64,37,2,128]{3,2,1,0:T(2,128)(2,1)S(1)}, u32[]{:S(2)}, u32[]{:S(2)}) async-start(bf16[64,37,2,128]{3,2,1,0:T(2,128)(2,1)} %bitcast.14), calls=%async_computation | async-start | bytes 2424832 | tf_op jit(solution)/shard_map/all_to_all | solution.py:283
  52.2 37.4 %all-to-all-start.1 = ((f16[512,4,128]{2,1,0:T(4,128)(2,1)}), f16[512,4,128]{2,1,0:T(4,128)(2,1)S(1)}, u32[]{:S(2)}, u32[]{:S(2)}) async-start(f16[512,4,128]{2,1,0:T(4,128)(2,1)} %bitcast.5), calls=%async_computation.1 | async-start | bytes 1048576 | tf_op jit(solution)/shard_map/all_to_all | solution.py:290
